TPU v7x, 256 devices: a whole 4x4x8 slice. The times are simulated.
256 devices in a mesh: section: 2 (over y_hi), dp: 16 (over z, core), vocab: 8 (over y_lo, x).
Axes of the slice: x: 4, y: 4 (y_hi: 2, y_lo: 2; y = y_hi * 2 + y_lo), z: 8, core: 2. Of those that a mesh axis runs over, the one named last changes fastest.
Arguments:
- activations: bfloat16 [2, 2048, 2048], P('section', 'dp'), may hold values from -32 to 32
- token_ids: int32 [2, 2048], replicated, may hold values from 0 to 65535
- embed_table: bfloat16 [65536, 2048], P(('dp', 'vocab')), may hold values from -3 to 3
Outputs:
- tied_grad: bfloat16 [128, 2, 256, 2048], P(('dp', 'vocab'), 'section')
All inputs are finite; a program needn't handle non-finite values.
Results may differ from a plain program's by a relative error of at most 0.0029.
Values may be sent and summed in bfloat16 or wider, within the bound.
No kernel may reach another device: no remote copies, remote signals or barrier semaphores. Data moves between devices by JAX's collectives and lax.ppermute only.
A program may use at most 128 MiB of HBM per device.

v0:
```python
import jax
import jax.numpy as jnp
import numpy as np
from jax import lax
from jax.experimental import pallas as pl
from jax.experimental.pallas import tpu as pltpu
from jax.sharding import Mesh
from jax.sharding import PartitionSpec as P


AXES = ("s", "z", "c", "u", "x")
SUBS = 2
SLOTS = 8
CHUNK = 512


def sizes():
    return {a: lax.axis_size(a) for a in AXES}


def moved(block, route):
    n = sizes()
    shape = [n[a] for a in AXES]
    pairs = []
    for at in np.ndindex(*shape):
        to = route(dict(zip(AXES, at)))
        to = tuple(to[a] % n[a] for a in AXES)
        pairs.append((int(np.ravel_multi_index(at, shape)), int(np.ravel_multi_index(to, shape))))
    return lax.ppermute(block, AXES, pairs)


def across(d):
    return {**d, "s": 1 - d["s"], "u": 1 - d["u"]}


def along_z(d):
    return {**d, "z": d["z"] + (1 if (d["x"] + d["c"]) % 2 == 0 else -1)}


def along_x(d):
    return {**d, "x": d["x"] + (-1 if d["c"] == 0 else 1)}


def other_core(d):
    return {**d, "c": 1 - d["c"]}


def plus_z(d):
    return {**d, "z": d["z"] + 1}


def picked(table, index):
    hit = index[:, None] == jnp.arange(table.shape[0], dtype=jnp.int32)[None, :]
    hit = hit.reshape(hit.shape + (1,) * (table.ndim - 1))
    return jnp.sum(jnp.where(hit, table[None], jnp.zeros((), table.dtype)), axis=1)


def shared(value, axes):
    count = lax.axis_size(axes)
    return lax.all_to_all(jnp.broadcast_to(value, (count, *value.shape)), axes, 0, 0, tiled=True)


def joined(pairs):
    peak = jnp.max(pairs[:, 0], axis=0)
    total = jnp.sum(pairs[:, 1] * jnp.exp(pairs[:, 0] - peak[None]), axis=0)
    return jnp.stack([peak, total])


def dot(a, b, dims):
    return lax.dot_general(a, b, (dims, ((), ())), preferred_element_type=jnp.float32)


def anywhere(count):
    return [pl.BlockSpec(memory_space=pl.ANY)] * count


def in_vmem(count):
    return [pl.BlockSpec(memory_space=pltpu.VMEM)] * count


def fetch(sources, targets, sems):
    copies = [pltpu.make_async_copy(a, b, sems.at[k]) for k, (a, b) in enumerate(zip(sources, targets))]
    for copy in copies:
        copy.start()
    return copies


def await_rows(ref, each, count, k, sems, first):
    for j in range(count):
        piece = k * count + j
        view = ref.at[pl.ds(pl.multiple_of(piece * each, each), each), :]
        pltpu.make_async_copy(view, view, sems.at[first + piece]).wait()


def stacked(ref, parts):
    at, views = 0, []
    for part in parts:
        views.append(ref.at[pl.ds(at, part.shape[0]), :])
        at += part.shape[0]
    return views


def score_kernel(count, refs):
    start, table, parts = refs[0], refs[1], refs[2 : 2 + count]
    scores, stats, table_here, rows_here, sems = refs[2 + count :]
    lines = table_here.shape[0]
    mine = table.at[pl.ds(pl.multiple_of(start[0], lines), lines), :]
    copies = fetch([mine, *parts], [table_here, *stacked(rows_here, parts)], sems)
    copies[0].wait()
    each = parts[0].shape[0]

    def step(k, carry):
        await_rows(rows_here, each, CHUNK // each, k, sems, 1)
        at = pl.ds(pl.multiple_of(k * CHUNK, CHUNK), CHUNK)
        value = lax.dot_general(
            table_here[...], rows_here[at, :], (((1,), (1,)), ((), ())), preferred_element_type=jnp.float32
        )
        scores[:, at] = value
        peak = jnp.max(value, axis=0, keepdims=True)
        stats[0:1, at] = peak
        stats[1:2, at] = jnp.sum(jnp.exp(value - peak), axis=0, keepdims=True)
        return carry

    lax.fori_loop(0, rows_here.shape[0] // CHUNK, step, 0)


def scored(start, lines, table, parts):
    count = sum(p.shape[0] for p in parts)
    width = table.shape[1]
    return pl.pallas_call(
        lambda *refs: score_kernel(len(parts), refs),
        out_shape=[
            jax.ShapeDtypeStruct((lines, count), jnp.float32),
            jax.ShapeDtypeStruct((2, count), jnp.float32),
        ],
        in_specs=[pl.BlockSpec(memory_space=pltpu.SMEM)] + anywhere(1 + len(parts)),
        out_specs=in_vmem(2),
        scratch_shapes=[
            pltpu.VMEM((lines, width), table.dtype),
            pltpu.VMEM((count, width), table.dtype),
            pltpu.SemaphoreType.DMA((1 + len(parts),)),
        ],
        cost_estimate=pl.CostEstimate(
            flops=2 * count * lines * width, bytes_accessed=2 * width * (lines + count), transcendentals=0
        ),
        name="score",
    )(start.reshape(1), table, *parts)


def gradient_kernel(tables, count, refs):
    base, peak, total, targets, slots = refs[:5]
    gots, scores = refs[5:7], refs[7 : 7 + tables]
    parts = refs[7 + tables : 7 + tables + count]
    out, scores_here, rows_here, got_here, result, outgoing, sems = refs[7 + tables + count :]
    lines, width = out.shape
    at, views = 0, []
    for table in scores:
        views.append(scores_here.at[:, pl.ds(at, table.shape[1])])
        at += table.shape[1]
    copies = fetch(
        [*scores, *gots, *parts], views + stacked(got_here, gots) + stacked(rows_here, parts), sems
    )
    for copy in copies[: tables + 2]:
        copy.wait()
    row = base[0] + lax.broadcasted_iota(jnp.int32, (lines, 1), 0)
    first = jnp.where(row == slots[...], 1.0, 0.0).astype(got_here.dtype)
    span = outgoing.shape[2]
    columns = [slice(k * span, (k + 1) * span) for k in range(width // span)]
    for cols in columns:
        result[:, cols] = jnp.dot(first, got_here[:, cols], preferred_element_type=jnp.float32)
    each = parts[0].shape[0]

    def step(k, carry):
        await_rows(rows_here, each, CHUNK // each, k, sems, tables + 2)
        at = pl.ds(pl.multiple_of(k * CHUNK, CHUNK), CHUNK)
        hot = jnp.where(row == targets[:, at], 1.0, 0.0)
        soft = jnp.exp(scores_here[:, at] - peak[:, at]) * (1.0 / total[:, at])
        weights = (soft - hot).astype(rows_here.dtype)
        for cols in columns:
            result[:, cols] += jnp.dot(weights, rows_here[at, cols], preferred_element_type=jnp.float32)
        return carry

    lax.fori_loop(0, rows_here.shape[0] // CHUNK, step, 0)
    stores = []
    for k, cols in enumerate(columns):
        outgoing[k] = result[:, cols].astype(out.dtype)
        store = pltpu.make_async_copy(
            outgoing.at[k], out.at[:, pl.ds(k * span, span)], sems.at[len(copies) + k]
        )
        store.start()
        stores.append(store)
    for store in stores:
        store.wait()


def gradient(dtype, lines, base, scores, parts, peak, total, targets, slots, gots):
    tokens, width = peak.shape[1], gots[0].shape[1]
    step = width // 4
    return pl.pallas_call(
        lambda *refs: gradient_kernel(len(scores), len(parts), refs),
        out_shape=jax.ShapeDtypeStruct((lines, width), dtype),
        in_specs=[pl.BlockSpec(memory_space=pltpu.SMEM)] + in_vmem(4) + anywhere(2 + len(scores) + len(parts)),
        out_specs=pl.BlockSpec(memory_space=pl.ANY),
        scratch_shapes=[
            pltpu.VMEM((lines, tokens), jnp.float32),
            pltpu.VMEM((tokens, width), jnp.bfloat16),
            pltpu.VMEM((2 * gots[0].shape[0], width), jnp.bfloat16),
            pltpu.VMEM((lines, width), jnp.float32),
            pltpu.VMEM((width // step, lines, step), dtype),
            pltpu.SemaphoreType.DMA((2 + len(scores) + len(parts) + width // step,)),
        ],
        cost_estimate=pl.CostEstimate(
            flops=2 * tokens * lines * width, bytes_accessed=2 * width * tokens, transcendentals=lines * tokens
        ),
        name="gradient",
    )(base.reshape(1), peak, total, targets, slots, *gots, *scores, *parts)


def whole(activations, token_ids, embed_table):
    own_rows = activations[0]
    rows, width = own_rows.shape
    n = sizes()
    nz, nc = n["z"], n["c"]
    s, z, c, u, x = (lax.axis_index(a) for a in AXES)
    column = u * n["x"] + x
    columns = n["u"] * n["x"]
    table_count = embed_table.shape[0]
    half = table_count // n["s"]

    cut = rows // SUBS
    blocks, cots = [], []
    for k in range(SUBS):
        piece = own_rows[k * cut : (k + 1) * cut]
        partner = moved(piece, across)
        if blocks:
            partner, blocks[-1] = lax.optimization_barrier((partner, blocks[-1]))
        blocks.append(jnp.where(s == 0, partner, piece))
        cots.append(jnp.where(s == 0, piece, partner))
    cot = jnp.concatenate(cots, axis=0)

    hops = np.array([0, 1] + [h for step in range(2, nz // 2 + 1) for h in (step, 1 - step)], np.int32)
    way = jnp.where((x + c) % 2 == 0, 1, -1)
    order = []
    for k in range(0, len(hops), 2):
        near = hops[k : k + 2]
        order += [(z - way * near) % nz, (z + way * near) % nz + nz]
    order = jnp.concatenate(order)
    shards = nz * nc

    def both_cores(table):
        table = table.reshape(nz, nc, rows)
        mine = jnp.arange(nc, dtype=jnp.int32)[None, :, None] == c
        return jnp.concatenate(
            [jnp.sum(jnp.where(hit, table, 0), axis=1) for hit in (mine, ~mine)], axis=0
        )

    shard_in, shard_out = both_cores(token_ids[0].reshape(shards, rows)), both_cores(
        token_ids[1].reshape(shards, rows)
    )
    targets = picked(shard_out, order).reshape(1, shards * rows)
    base = ((z * nc + c) * columns + column) * table_count + s * half

    per_z = nc * columns * table_count
    cell_of = lambda v: (v // per_z, (v // table_count) % columns, (v // half) % n["s"])
    before = (
        jnp.arange(rows)[:, None] < jnp.arange(rows)[None, :]
    ).astype(jnp.bfloat16)

    def ranks(match):
        return dot(match.astype(jnp.bfloat16), before, ((1,), (0,))).astype(jnp.int32)

    slot = jnp.arange(SLOTS, dtype=jnp.int32)
    shard_ids = picked(shard_in[:nz], z[None])[0]
    to_z, to_column, to_s = cell_of(shard_ids)
    here = (to_column == column) & (to_s == s)
    out_match = (to_z[None, :] == jnp.arange(nz)[:, None]) & here[None, :]
    out_rank = ranks(out_match)
    every = token_ids[0].reshape(nz * nc, rows)
    cz, cc, cs = cell_of(every)
    cell = (cz * columns + cc) * n["s"] + cs
    cells = nz * columns * n["s"]
    held = jnp.sum(
        (cell[:, :, None] == jnp.arange(cells, dtype=jnp.int32)[None, None, :]).astype(jnp.int32), axis=1
    )
    crowded = jnp.max(held) > SLOTS

    cot, crowded = lax.optimization_barrier((cot, crowded))
    choose = out_match[:, None, :] & (out_rank[:, None, :] == slot[None, :, None])
    sent = dot(choose.reshape(nz * SLOTS, rows).astype(jnp.bfloat16), cot, ((1,), (0,)))
    sent = sent.astype(jnp.bfloat16)
    from_z, from_column, from_s = cell_of(shard_in)
    in_match = (from_z == z) & (from_column == column) & (from_s == s)
    in_rank = ranks(in_match)
    filled = in_match[:, None, :] & (in_rank[:, None, :] == slot[None, :, None])
    slots = jnp.sum(jnp.where(filled, shard_in[:, None, :] + 1, 0), axis=2).reshape(1, shards * SLOTS) - 1

    got = lax.all_to_all(sent, "z", 0, 0, tiled=True)

    there, back = [[block] for block in blocks], [[] for _ in blocks]
    for step in range(1, nz // 2 + 1):
        for k in range(SUBS):
            block = there[k][-1]
            there[k].append(moved(block, along_z))
            if step > 1:
                back[k].append(moved(block, along_x))
    parts = []
    for pair in range(0, len(hops), 2):
        group = []
        for hop in hops[pair : pair + 2]:
            group += [there[k][hop] if hop >= 0 else back[k][-hop - 1] for k in range(SUBS)]
        parts += group + [moved(p, other_core) for p in group]
    table_scores, stats = scored(s * half, half, embed_table, parts)
    stats, got = lax.optimization_barrier((stats, got))
    scores = [table_scores]
    gots = (got, moved(got, other_core))

    local = stats.reshape(2, shards, rows)
    place = jnp.arange(shards, dtype=jnp.int32)
    inverse = jnp.sum(jnp.where(order[None, :] == place[:, None], place[None, :], 0), axis=1)
    near = jnp.stack([picked(local[0], inverse[:nz]), picked(local[1], inverse[:nz])])
    far = jnp.stack([picked(local[0], inverse[nz:]), picked(local[1], inverse[nz:])])
    pair = joined(jnp.stack([near, moved(far, other_core)]))
    pair = joined(shared(pair, ("s", "u", "x")))
    pair = joined(shared(pair, "z"))
    pair = jnp.concatenate([pair, moved(pair, other_core)], axis=1)
    peak_all = picked(pair[0], order).reshape(1, shards * rows)
    total_all = picked(pair[1], order).reshape(1, shards * rows)

    def plain(cot, token_ids, args):
        return gradient(jnp.bfloat16, half, *args)

    def crowded_too(cot, token_ids, args):
        my_rows = base + jnp.arange(half, dtype=jnp.int32)

        def step(k, carry):
            total, block = carry
            shard = (z - k) % nz
            for core in range(2):
                if core == 1:
                    block = moved(block, other_core)
                owner = c if core == 0 else 1 - c
                shard_ids = lax.dynamic_slice(
                    token_ids[0].reshape(nz, nc, rows), (shard, owner, 0), (1, 1, rows)
                ).reshape(rows)
                a, b, d = cell_of(shard_ids)
                match = (a == z) & (b == column) & (d == s)
                late = match & (ranks(match[None])[0] >= SLOTS)
                weights = (my_rows[:, None] == jnp.where(late, shard_ids, -1)[None, :]).astype(jnp.bfloat16)
                total = total + dot(weights, block, ((1,), (0,)))
            block = moved(moved(block, other_core), plus_z)
            return total, block

        total, _ = lax.fori_loop(0, nz, step, (gradient(jnp.float32, half, *args), cot))
        return total.astype(jnp.bfloat16)

    args = (base, scores, parts, peak_all, total_all, targets, slots, gots)
    out = lax.cond(crowded, crowded_too, plain, cot, token_ids, args)
    return out.reshape(1, 1, half, width)


def solution(mesh):
    finer = Mesh(mesh.devices.reshape(mesh.shape["section"], 8, 2, 2, 4), AXES)
    in_specs = (P("s", ("z", "c"), None), P(), P(("z", "c", "u", "x"), None))
    out_specs = P(("z", "c", "u", "x"), "s", None, None)
    return jax.shard_map(whole, mesh=finer, in_specs=in_specs, out_specs=out_specs, check_vma=False)
```

profile of v0, /device:TPU:1, one launch (start us, length us, event | category | flops | bytes accessed | tf_op | source)
XLA Modules:
  0.0 118.4 jit_solution(1193787400926608279)
XLA Ops:
  0.0 1.1 slice_bitcast_fusion.1
  1.1 3.6 %collective-permute-start.3 = (bf16[64,2048]{1,0:T(8,128)(2,1)S(1)}, bf16[64,2048]{1,0:T(8,128)(2,1)S(1)}, u32[]{:S(2)}, u32[]{:S(2)}) collective-permute-start(bf16[64,2048]{1,0:T(8,128)(2,1)S(1)} %get-tuple-element.681), channel_id=1, source_target_pairs={{0,132},{1,133},{2,134},{3,135},{4,128},{5,129},{6,130},{7,131},{8... | collective-permute-start | bytes 786440 | tf_op jit(solution)/shard_map/ppermute | solution.py:29
  8.2 1.5 %collective-permute-done.3 = bf16[64,2048]{1,0:T(8,128)(2,1)S(1)} collective-permute-done((bf16[64,2048]{1,0:T(8,128)(2,1)S(1)}, bf16[64,2048]{1,0:T(8,128)(2,1)S(1)}, u32[]{:S(2)}, u32[]{:S(2)}) %collective-permute-start.3) | collective-permute-done | bytes 262176 | tf_op jit(solution)/shard_map/ppermute | solution.py:29
  9.8 1.7 %broadcast_select_fusion.3 = (bf16[64,2048]{1,0:T(8,128)(2,1)}, bf16[64,2048]{1,0:T(8,128)(2,1)S(1)}) fusion(bf16[64,2048]{1,0:T(8,128)(2,1)S(1)} %collective-permute-done.3, pred[]{:T(512)S(6)} %eq.502, bf16[1,128,2048]{2,1,0:T(8,128)(2,1)} %param.11), kind=kLoop, calls=%fused_computation.153 | loop fusion | flops 262144 | bytes 1048577 | tf_op jit(solution)/shard_map/jit(_where)/select_n | solution.py:238
  11.5 3.9 %collective-permute-done.4 = bf16[64,2048]{1,0:T(8,128)(2,1)S(1)} collective-permute-done((bf16[64,2048]{1,0:T(8,128)(2,1)S(1)}, bf16[64,2048]{1,0:T(8,128)(2,1)S(1)}, u32[]{:S(2)}, u32[]{:S(2)}) %collective-permute-start.4) | collective-permute-done | bytes 262176 | tf_op jit(solution)/shard_map/ppermute | solution.py:29
  16.1 6.4 %collective-permute-start.6 = (bf16[64,2048]{1,0:T(8,128)(2,1)S(1)}, bf16[64,2048]{1,0:T(8,128)(2,1)S(1)}, u32[]{:S(2)}, u32[]{:S(2)}) collective-permute-start(bf16[64,2048]{1,0:T(8,128)(2,1)S(1)} %get-tuple-element.677.refs_3_), channel_id=1, source_target_pairs={{0,16},{1,113},{2,18},{3,115},{4,20},{5,117},{6,22},{7,119},{8,120... | collective-permute-start | bytes 786440 | tf_op jit(solution)/shard_map/ppermute | solution.py:29
  22.6 1.5 %collective-permute-start.5 = (bf16[64,2048]{1,0:T(8,128)(2,1)S(1)}, bf16[64,2048]{1,0:T(8,128)(2,1)S(1)}, u32[]{:S(2)}, u32[]{:S(2)}) collective-permute-start(bf16[64,2048]{1,0:T(8,128)(2,1)S(1)} %get-tuple-element.605.refs_2_), channel_id=1, source_target_pairs={{0,16},{1,113},{2,18},{3,115},{4,20},{5,117},{6,22},{7,119},{8,120... | collective-permute-start | bytes 786440 | tf_op jit(solution)/shard_map/ppermute | solution.py:29
  24.1 1.7 %collective-permute-done.6.refs_5_ = bf16[64,2048]{1,0:T(8,128)(2,1)S(1)} collective-permute-done((bf16[64,2048]{1,0:T(8,128)(2,1)S(1)}, bf16[64,2048]{1,0:T(8,128)(2,1)S(1)}, u32[]{:S(2)}, u32[]{:S(2)}) %collective-permute-start.6) | collective-permute-done | bytes 262176 | tf_op jit(solution)/shard_map/ppermute | solution.py:29
  25.8 3.1 %collective-permute-start.12 = (bf16[64,2048]{1,0:T(8,128)(2,1)S(1)}, bf16[64,2048]{1,0:T(8,128)(2,1)S(1)}, u32[]{:S(2)}, u32[]{:S(2)}) collective-permute-start(bf16[64,2048]{1,0:T(8,128)(2,1)S(1)} %collective-permute-done.6.refs_5_), channel_id=1, source_target_pairs={{0,16},{1,113},{2,18},{3,115},{4,20},{5,117},{6,22},{7,119},{8,120... | collective-permute-start | bytes 786440 | tf_op jit(solution)/shard_map/ppermute | solution.py:29
  29.1 5.6 %collective-permute-start.10 = (bf16[64,2048]{1,0:T(8,128)(2,1)S(1)}, bf16[64,2048]{1,0:T(8,128)(2,1)S(1)}, u32[]{:S(2)}, u32[]{:S(2)}) collective-permute-start(bf16[64,2048]{1,0:T(8,128)(2,1)S(1)} %collective-permute-done.6.refs_5_), channel_id=1, source_target_pairs={{0,8},{1,9},{2,10},{3,11},{4,12},{5,13},{6,14},{7,15},{8,0},{9,1},... | collective-permute-start | bytes 786440 | tf_op jit(solution)/shard_map/ppermute | solution.py:29
  35.5 2.1 %collective-permute-start.9 = (bf16[64,2048]{1,0:T(8,128)(2,1)S(1)}, bf16[64,2048]{1,0:T(8,128)(2,1)S(1)}, u32[]{:S(2)}, u32[]{:S(2)}) collective-permute-start(bf16[64,2048]{1,0:T(8,128)(2,1)S(1)} %collective-permute-done.5.refs_4_), channel_id=1, source_target_pairs={{0,8},{1,9},{2,10},{3,11},{4,12},{5,13},{6,14},{7,15},{8,0},{9,1},... | collective-permute-start | bytes 786440 | tf_op jit(solution)/shard_map/ppermute | solution.py:29
  38.0 2.3 %collective-permute-done.11.refs_10_ = bf16[64,2048]{1,0:T(8,128)(2,1)S(1)} collective-permute-done((bf16[64,2048]{1,0:T(8,128)(2,1)S(1)}, bf16[64,2048]{1,0:T(8,128)(2,1)S(1)}, u32[]{:S(2)}, u32[]{:S(2)}) %collective-permute-start.11) | collective-permute-done | bytes 262176 | tf_op jit(solution)/shard_map/ppermute | solution.py:29
  41.2 4.0 %collective-permute-start.16 = (bf16[64,2048]{1,0:T(8,128)(2,1)S(1)}, bf16[64,2048]{1,0:T(8,128)(2,1)S(1)}, u32[]{:S(2)}, u32[]{:S(2)}) collective-permute-start(bf16[64,2048]{1,0:T(8,128)(2,1)S(1)} %collective-permute-done.12.refs_11_), channel_id=1, source_target_pairs={{0,8},{1,9},{2,10},{3,11},{4,12},{5,13},{6,14},{7,15},{8,0},{9,1},... | collective-permute-start | bytes 786440 | tf_op jit(solution)/shard_map/ppermute | solution.py:29
  46.0 2.1 %collective-permute-start.21 = (bf16[64,2048]{1,0:T(8,128)(2,1)S(1)}, bf16[64,2048]{1,0:T(8,128)(2,1)S(1)}, u32[]{:S(2)}, u32[]{:S(2)}) collective-permute-start(bf16[64,2048]{1,0:T(8,128)(2,1)S(1)} %collective-permute-done.11.refs_10_), channel_id=1, source_target_pairs={{0,3},{1,0},{2,1},{3,2},{4,7},{5,4},{6,5},{7,6},{8,9},{9,10},{10,1... | collective-permute-start | bytes 786440 | tf_op jit(solution)/shard_map/ppermute | solution.py:29
  48.0 2.1 %collective-permute-start.15 = (bf16[64,2048]{1,0:T(8,128)(2,1)S(1)}, bf16[64,2048]{1,0:T(8,128)(2,1)S(1)}, u32[]{:S(2)}, u32[]{:S(2)}) collective-permute-start(bf16[64,2048]{1,0:T(8,128)(2,1)S(1)} %collective-permute-done.11.refs_10_), channel_id=1, source_target_pairs={{0,8},{1,9},{2,10},{3,11},{4,12},{5,13},{6,14},{7,15},{8,0},{9,1},... | collective-permute-start | bytes 786440 | tf_op jit(solution)/shard_map/ppermute | solution.py:29
  50.7 1.9 %collective-permute-start.28 = (bf16[64,2048]{1,0:T(8,128)(2,1)S(1)}, bf16[64,2048]{1,0:T(8,128)(2,1)S(1)}, u32[]{:S(2)}, u32[]{:S(2)}) collective-permute-start(bf16[64,2048]{1,0:T(8,128)(2,1)S(1)} %collective-permute-done.20.refs_19_), channel_id=1, source_target_pairs={{0,16},{1,113},{2,18},{3,115},{4,20},{5,117},{6,22},{7,119},{8,120... | collective-permute-start | bytes 786440 | tf_op jit(solution)/shard_map/ppermute | solution.py:29
  54.7 2.4 %collective-permute-start.24 = (bf16[64,2048]{1,0:T(8,128)(2,1)S(1)}, bf16[64,2048]{1,0:T(8,128)(2,1)}, u32[]{:S(2)}, u32[]{:S(2)}) collective-permute-start(bf16[64,2048]{1,0:T(8,128)(2,1)S(1)} %collective-permute-done.20.refs_19_), channel_id=1, source_target_pairs={{0,8},{1,9},{2,10},{3,11},{4,12},{5,13},{6,14},{7,15},{8,0},{9,1},... | collective-permute-start | bytes 786440 | tf_op jit(solution)/shard_map/ppermute | solution.py:29
  58.0 2.4 %collective-permute-start.23 = (bf16[64,2048]{1,0:T(8,128)(2,1)S(1)}, bf16[64,2048]{1,0:T(8,128)(2,1)}, u32[]{:S(2)}, u32[]{:S(2)}) collective-permute-start(bf16[64,2048]{1,0:T(8,128)(2,1)S(1)} %collective-permute-done.19.refs_18_), channel_id=1, source_target_pairs={{0,8},{1,9},{2,10},{3,11},{4,12},{5,13},{6,14},{7,15},{8,0},{9,1},... | collective-permute-start | bytes 786440 | tf_op jit(solution)/shard_map/ppermute | solution.py:29
  60.6 1.1 pad_maximum_fusion
  62.6 3.7 %all-to-all-start = ((bf16[8,8,2048]{2,1,0:T(8,128)(2,1)}), bf16[8,8,2048]{2,1,0:T(8,128)(2,1)S(1)}, u32[]{:S(2)}, u32[]{:S(2)}) async-start(bf16[8,8,2048]{2,1,0:T(8,128)(2,1)} %fusion.102), calls=%async_computation | async-start | bytes 524288 | tf_op jit(solution)/shard_map/all_to_all | solution.py:297
  70.0 6.0 %score.1 = (f32[256,2048]{1,0:T(8,128)S(1)}, f32[2,2048]{1,0:T(2,128)}) custom-call(s32[1]{0:T(128)} %bitcast.7.refs_0_, bf16[512,2048]{1,0:T(8,128)(2,1)} %refs_1_.1, bf16[64,2048]{1,0:T(8,128)(2,1)S(1)} %get-tuple-element.605.refs_2_, bf16[64,2048]{1,0:T(8,128)(2,1)S(1)} %get-tuple-element.677.refs_3_, bf16[64,2048]{1,0:T(8,128)(2,1)} %copy-done.3, ...), custom_call_target="tpu_custom_call" | custom-call | flops 2147483648 | bytes 9437184 | tf_op jit(solution)/shard_map/score/pallas_call | solution.py:130
  76.1 1.2 %all-to-all-done = bf16[8,8,2048]{2,1,0:T(8,128)(2,1)S(1)} async-done(((bf16[8,8,2048]{2,1,0:T(8,128)(2,1)}), bf16[8,8,2048]{2,1,0:T(8,128)(2,1)S(1)}, u32[]{:S(2)}, u32[]{:S(2)}) %all-to-all-start) | async-done | bytes 262176 | tf_op jit(solution)/shard_map/all_to_all | solution.py:297
  78.3 2.0 %collective-permute-start.35 = (f32[2,8,128]{2,1,0:T(8,128)S(1)}, f32[2,8,128]{2,1,0:T(8,128)S(1)}, u32[]{:S(2)}, u32[]{:S(2)}) collective-permute-start(f32[2,8,128]{2,1,0:T(8,128)S(1)} %pad_maximum_fusion.3), channel_id=1, source_target_pairs={{0,8},{1,9},{2,10},{3,11},{4,12},{5,13},{6,14},{7,15},{8,0},{9,1},... | collective-permute-start | bytes 24584 | tf_op jit(solution)/shard_map/ppermute | solution.py:29
  81.8 6.2 %all-to-all-start.1 = ((f32[16,2,8,128]{3,2,1,0:T(8,128)}), f32[16,2,8,128]{3,2,1,0:T(8,128)S(1)}, u32[]{:S(2)}, u32[]{:S(2)}) async-start(f32[16,2,8,128]{3,2,1,0:T(8,128)} %broadcast_in_dim.239), calls=%async_computation.1 | async-start | bytes 262144 | tf_op jit(solution)/shard_map/all_to_all | solution.py:60
  88.0 1.3 %iota_compare_fusion.6 = pred[16,16]{1,0:T(8,128)(4,1)} fusion(s32[16]{0:T(128)} %copy-done.22), kind=kLoop, calls=%fused_computation.260 | loop fusion | flops 256 | bytes 320 | tf_op jit(solution)/shard_map/eq | solution.py:53
  89.3 1.3 %pad_add_fusion = s32[16,128]{1,0:T(8,128)} fusion(s32[8,128]{1,0:T(8,128)} %get-tuple-element.642, s32[8,128]{1,0:T(8,128)} %get-tuple-element.641), kind=kLoop, calls=%fused_computation.248 | loop fusion | flops 2048 | bytes 16384 | tf_op jit(solution)/shard_map/concatenate | solution.py:253
  90.5 4.3 %all-to-all-done.1 = f32[16,2,8,128]{3,2,1,0:T(8,128)S(1)} async-done(((f32[16,2,8,128]{3,2,1,0:T(8,128)}), f32[16,2,8,128]{3,2,1,0:T(8,128)S(1)}, u32[]{:S(2)}, u32[]{:S(2)}) %all-to-all-start.1) | async-done | bytes 131104 | tf_op jit(solution)/shard_map/all_to_all | solution.py:60
  95.5 3.7 %all-to-all-start.2 = ((f32[8,2,8,128]{3,2,1,0:T(8,128)}), f32[8,2,8,128]{3,2,1,0:T(8,128)S(1)}, u32[]{:S(2)}, u32[]{:S(2)}) async-start(f32[8,2,8,128]{3,2,1,0:T(8,128)} %broadcast_in_dim.240), calls=%async_computation.2 | async-start | bytes 131072 | tf_op jit(solution)/shard_map/all_to_all | solution.py:60
  100.1 6.4 %all-to-all-done.2 = f32[8,2,8,128]{3,2,1,0:T(8,128)S(1)} async-done(((f32[8,2,8,128]{3,2,1,0:T(8,128)}), f32[8,2,8,128]{3,2,1,0:T(8,128)S(1)}, u32[]{:S(2)}, u32[]{:S(2)}) %all-to-all-start.2) | async-done | bytes 65568 | tf_op jit(solution)/shard_map/all_to_all | solution.py:60
  106.5 3.3 %collective-permute-start.36 = (f32[2,8,128]{2,1,0:T(8,128)S(1)}, f32[2,8,128]{2,1,0:T(8,128)S(1)}, u32[]{:S(2)}, u32[]{:S(2)}) collective-permute-start(f32[2,8,128]{2,1,0:T(8,128)S(1)} %pad_maximum_fusion.6), channel_id=1, source_target_pairs={{0,8},{1,9},{2,10},{3,11},{4,12},{5,13},{6,14},{7,15},{8,0},{9,1},... | collective-permute-start | bytes 24584 | tf_op jit(solution)/shard_map/ppermute | solution.py:29
  112.4 5.9 %conditional.1 = (bf16[1,1,256,2048]{3,2,1,0:T(8,128)(2,1)}) conditional(s32[]{:T(128)} %convert_element_type.63, (s32[]{:T(128)}, f32[1,2048]{1,0:T(1,128)S(1)}, f32[1,2048]{1,0:T(1,128)S(1)}, s32[1,2048]{1,0:T(1,128)S(1)}, s32[1,128]{1,0:T(1,128)S(1)}, /*index=5*/bf16[64,2048]{1,0:T(8,128)(2,1)S(1)}, bf16[64,2048]{1,0:T(8,128)(2,1)}, ...), branch_computations={%region_22.23_spmd, %region_23.26_spmd} | conditional | flops 2417656064 | bytes 35751588 | solution.py:357
  112.4 5.9 %gradient.2 = bf16[256,2048]{1,0:T(8,128)(2,1)} custom-call(s32[1]{0:T(128)} %bitcast.refs_0_, f32[1,2048]{1,0:T(1,128)S(1)} %get-tuple-element.494.refs_1_, f32[1,2048]{1,0:T(1,128)S(1)} %get-tuple-element.495.refs_2_, s32[1,2048]{1,0:T(1,128)S(1)} %get-tuple-element.496.refs_3_, s32[1,128]{1,0:T(1,128)S(1)} %get-tuple-element.497.refs_4_, ...), custom_call_target="tpu_custom_call" | custom-call | flops 2147483648 | bytes 8388608 | tf_op jit(solution)/shard_map/cond/branch_0_fun/gradient/pallas_call | solution.py:199
  (146 shorter events, 21.4 us)
Async XLA Ops:
  1.1 8.6 %collective-permute-start.3 = (bf16[64,2048]{1,0:T(8,128)(2,1)S(1)}, bf16[64,2048]{1,0:T(8,128)(2,1)S(1)}, u32[]{:S(2)}, u32[]{:S(2)}) collective-permute-start(bf16[64,2048]{1,0:T(8,128)(2,1)S(1)} %get-tuple-element.681), channel_id=1, source_target_pairs={{0,132},{1,133},{2,134},{3,135},{4,128},{5,129},{6,130},{7,131},{8... | collective-permute-start | bytes 786440 | tf_op jit(solution)/shard_map/ppermute | solution.py:29
  4.8 10.6 %collective-permute-start.4 = (bf16[64,2048]{1,0:T(8,128)(2,1)S(1)}, bf16[64,2048]{1,0:T(8,128)(2,1)S(1)}, u32[]{:S(2)}, u32[]{:S(2)}) collective-permute-start(bf16[64,2048]{1,0:T(8,128)(2,1)S(1)} %get-tuple-element.682), channel_id=1, source_target_pairs={{0,132},{1,133},{2,134},{3,135},{4,128},{5,129},{6,130},{7,131},{8... | collective-permute-start | bytes 786440 | tf_op jit(solution)/shard_map/ppermute | solution.py:29
  16.1 9.7 %collective-permute-start.6 = (bf16[64,2048]{1,0:T(8,128)(2,1)S(1)}, bf16[64,2048]{1,0:T(8,128)(2,1)S(1)}, u32[]{:S(2)}, u32[]{:S(2)}) collective-permute-start(bf16[64,2048]{1,0:T(8,128)(2,1)S(1)} %get-tuple-element.677.refs_3_), channel_id=1, source_target_pairs={{0,16},{1,113},{2,18},{3,115},{4,20},{5,117},{6,22},{7,119},{8,120... | collective-permute-start | bytes 786440 | tf_op jit(solution)/shard_map/ppermute | solution.py:29
  22.6 12.2 %collective-permute-start.8 = (bf16[64,2048]{1,0:T(8,128)(2,1)S(1)}, bf16[64,2048]{1,0:T(8,128)(2,1)S(1)}, u32[]{:S(2)}, u32[]{:S(2)}) collective-permute-start(bf16[64,2048]{1,0:T(8,128)(2,1)S(1)} %get-tuple-element.677.refs_3_), channel_id=1, source_target_pairs={{0,8},{1,9},{2,10},{3,11},{4,12},{5,13},{6,14},{7,15},{8,0},{9,1},... | collective-permute-start | bytes 786440 | tf_op jit(solution)/shard_map/ppermute | solution.py:29
  22.6 6.5 %collective-permute-start.5 = (bf16[64,2048]{1,0:T(8,128)(2,1)S(1)}, bf16[64,2048]{1,0:T(8,128)(2,1)S(1)}, u32[]{:S(2)}, u32[]{:S(2)}) collective-permute-start(bf16[64,2048]{1,0:T(8,128)(2,1)S(1)} %get-tuple-element.605.refs_2_), channel_id=1, source_target_pairs={{0,16},{1,113},{2,18},{3,115},{4,20},{5,117},{6,22},{7,119},{8,120... | collective-permute-start | bytes 786440 | tf_op jit(solution)/shard_map/ppermute | solution.py:29
  24.1 10.7 %collective-permute-start.7 = (bf16[64,2048]{1,0:T(8,128)(2,1)S(1)}, bf16[64,2048]{1,0:T(8,128)(2,1)S(1)}, u32[]{:S(2)}, u32[]{:S(2)}) collective-permute-start(bf16[64,2048]{1,0:T(8,128)(2,1)S(1)} %get-tuple-element.605.refs_2_), channel_id=1, source_target_pairs={{0,8},{1,9},{2,10},{3,11},{4,12},{5,13},{6,14},{7,15},{8,0},{9,1},... | collective-permute-start | bytes 786440 | tf_op jit(solution)/shard_map/ppermute | solution.py:29
  25.8 9.0 %collective-permute-start.12 = (bf16[64,2048]{1,0:T(8,128)(2,1)S(1)}, bf16[64,2048]{1,0:T(8,128)(2,1)S(1)}, u32[]{:S(2)}, u32[]{:S(2)}) collective-permute-start(bf16[64,2048]{1,0:T(8,128)(2,1)S(1)} %collective-permute-done.6.refs_5_), channel_id=1, source_target_pairs={{0,16},{1,113},{2,18},{3,115},{4,20},{5,117},{6,22},{7,119},{8,120... | collective-permute-start | bytes 786440 | tf_op jit(solution)/shard_map/ppermute | solution.py:29
  29.0 12.2 %collective-permute-start.14 = (bf16[64,2048]{1,0:T(8,128)(2,1)S(1)}, bf16[64,2048]{1,0:T(8,128)(2,1)S(1)}, u32[]{:S(2)}, u32[]{:S(2)}) collective-permute-start(bf16[64,2048]{1,0:T(8,128)(2,1)S(1)} %collective-permute-done.6.refs_5_), channel_id=1, source_target_pairs={{0,3},{1,0},{2,1},{3,2},{4,7},{5,4},{6,5},{7,6},{8,9},{9,10},{10,1... | collective-permute-start | bytes 786440 | tf_op jit(solution)/shard_map/ppermute | solution.py:29
  29.1 12.1 %collective-permute-start.10 = (bf16[64,2048]{1,0:T(8,128)(2,1)S(1)}, bf16[64,2048]{1,0:T(8,128)(2,1)S(1)}, u32[]{:S(2)}, u32[]{:S(2)}) collective-permute-start(bf16[64,2048]{1,0:T(8,128)(2,1)S(1)} %collective-permute-done.6.refs_5_), channel_id=1, source_target_pairs={{0,8},{1,9},{2,10},{3,11},{4,12},{5,13},{6,14},{7,15},{8,0},{9,1},... | collective-permute-start | bytes 786440 | tf_op jit(solution)/shard_map/ppermute | solution.py:29
  34.7 5.5 %collective-permute-start.11 = (bf16[64,2048]{1,0:T(8,128)(2,1)S(1)}, bf16[64,2048]{1,0:T(8,128)(2,1)S(1)}, u32[]{:S(2)}, u32[]{:S(2)}) collective-permute-start(bf16[64,2048]{1,0:T(8,128)(2,1)S(1)} %collective-permute-done.5.refs_4_), channel_id=1, source_target_pairs={{0,16},{1,113},{2,18},{3,115},{4,20},{5,117},{6,22},{7,119},{8,120... | collective-permute-start | bytes 786440 | tf_op jit(solution)/shard_map/ppermute | solution.py:29
  34.8 10.4 %collective-permute-start.13 = (bf16[64,2048]{1,0:T(8,128)(2,1)S(1)}, bf16[64,2048]{1,0:T(8,128)(2,1)S(1)}, u32[]{:S(2)}, u32[]{:S(2)}) collective-permute-start(bf16[64,2048]{1,0:T(8,128)(2,1)S(1)} %collective-permute-done.5.refs_4_), channel_id=1, source_target_pairs={{0,3},{1,0},{2,1},{3,2},{4,7},{5,4},{6,5},{7,6},{8,9},{9,10},{10,1... | collective-permute-start | bytes 786440 | tf_op jit(solution)/shard_map/ppermute | solution.py:29
  35.5 10.0 %collective-permute-start.9 = (bf16[64,2048]{1,0:T(8,128)(2,1)S(1)}, bf16[64,2048]{1,0:T(8,128)(2,1)S(1)}, u32[]{:S(2)}, u32[]{:S(2)}) collective-permute-start(bf16[64,2048]{1,0:T(8,128)(2,1)S(1)} %collective-permute-done.5.refs_4_), channel_id=1, source_target_pairs={{0,8},{1,9},{2,10},{3,11},{4,12},{5,13},{6,14},{7,15},{8,0},{9,1},... | collective-permute-start | bytes 786440 | tf_op jit(solution)/shard_map/ppermute | solution.py:29
  40.3 5.7 %collective-permute-start.20 = (bf16[64,2048]{1,0:T(8,128)(2,1)S(1)}, bf16[64,2048]{1,0:T(8,128)(2,1)S(1)}, u32[]{:S(2)}, u32[]{:S(2)}) collective-permute-start(bf16[64,2048]{1,0:T(8,128)(2,1)S(1)} %collective-permute-done.12.refs_11_), channel_id=1, source_target_pairs={{0,16},{1,113},{2,18},{3,115},{4,20},{5,117},{6,22},{7,119},{8,120... | collective-permute-start | bytes 786440 | tf_op jit(solution)/shard_map/ppermute | solution.py:29
  41.2 6.9 %collective-permute-start.22 = (bf16[64,2048]{1,0:T(8,128)(2,1)S(1)}, bf16[64,2048]{1,0:T(8,128)(2,1)S(1)}, u32[]{:S(2)}, u32[]{:S(2)}) collective-permute-start(bf16[64,2048]{1,0:T(8,128)(2,1)S(1)} %collective-permute-done.12.refs_11_), channel_id=1, source_target_pairs={{0,3},{1,0},{2,1},{3,2},{4,7},{5,4},{6,5},{7,6},{8,9},{9,10},{10,1... | collective-permute-start | bytes 786440 | tf_op jit(solution)/shard_map/ppermute | solution.py:29
  41.2 8.9 %collective-permute-start.16 = (bf16[64,2048]{1,0:T(8,128)(2,1)S(1)}, bf16[64,2048]{1,0:T(8,128)(2,1)S(1)}, u32[]{:S(2)}, u32[]{:S(2)}) collective-permute-start(bf16[64,2048]{1,0:T(8,128)(2,1)S(1)} %collective-permute-done.12.refs_11_), channel_id=1, source_target_pairs={{0,8},{1,9},{2,10},{3,11},{4,12},{5,13},{6,14},{7,15},{8,0},{9,1},... | collective-permute-start | bytes 786440 | tf_op jit(solution)/shard_map/ppermute | solution.py:29
  45.2 5.5 %collective-permute-start.19 = (bf16[64,2048]{1,0:T(8,128)(2,1)S(1)}, bf16[64,2048]{1,0:T(8,128)(2,1)S(1)}, u32[]{:S(2)}, u32[]{:S(2)}) collective-permute-start(bf16[64,2048]{1,0:T(8,128)(2,1)S(1)} %collective-permute-done.11.refs_10_), channel_id=1, source_target_pairs={{0,16},{1,113},{2,18},{3,115},{4,20},{5,117},{6,22},{7,119},{8,120... | collective-permute-start | bytes 786440 | tf_op jit(solution)/shard_map/ppermute | solution.py:29
  45.5 7.1 %collective-permute-start.18 = (bf16[64,2048]{1,0:T(8,128)(2,1)S(1)}, bf16[64,2048]{1,0:T(8,128)(2,1)S(1)}, u32[]{:S(2)}, u32[]{:S(2)}) collective-permute-start(bf16[64,2048]{1,0:T(8,128)(2,1)S(1)} %collective-permute-done.14.refs_13_), channel_id=1, source_target_pairs={{0,8},{1,9},{2,10},{3,11},{4,12},{5,13},{6,14},{7,15},{8,0},{9,1},... | collective-permute-start | bytes 786440 | tf_op jit(solution)/shard_map/ppermute | solution.py:29
  46.0 8.7 %collective-permute-start.21 = (bf16[64,2048]{1,0:T(8,128)(2,1)S(1)}, bf16[64,2048]{1,0:T(8,128)(2,1)S(1)}, u32[]{:S(2)}, u32[]{:S(2)}) collective-permute-start(bf16[64,2048]{1,0:T(8,128)(2,1)S(1)} %collective-permute-done.11.refs_10_), channel_id=1, source_target_pairs={{0,3},{1,0},{2,1},{3,2},{4,7},{5,4},{6,5},{7,6},{8,9},{9,10},{10,1... | collective-permute-start | bytes 786440 | tf_op jit(solution)/shard_map/ppermute | solution.py:29
  48.0 9.0 %collective-permute-start.15 = (bf16[64,2048]{1,0:T(8,128)(2,1)S(1)}, bf16[64,2048]{1,0:T(8,128)(2,1)S(1)}, u32[]{:S(2)}, u32[]{:S(2)}) collective-permute-start(bf16[64,2048]{1,0:T(8,128)(2,1)S(1)} %collective-permute-done.11.refs_10_), channel_id=1, source_target_pairs={{0,8},{1,9},{2,10},{3,11},{4,12},{5,13},{6,14},{7,15},{8,0},{9,1},... | collective-permute-start | bytes 786440 | tf_op jit(solution)/shard_map/ppermute | solution.py:29
  50.1 7.9 %collective-permute-start.17 = (bf16[64,2048]{1,0:T(8,128)(2,1)S(1)}, bf16[64,2048]{1,0:T(8,128)(2,1)S(1)}, u32[]{:S(2)}, u32[]{:S(2)}) collective-permute-start(bf16[64,2048]{1,0:T(8,128)(2,1)S(1)} %collective-permute-done.13.refs_12_), channel_id=1, source_target_pairs={{0,8},{1,9},{2,10},{3,11},{4,12},{5,13},{6,14},{7,15},{8,0},{9,1},... | collective-permute-start | bytes 786440 | tf_op jit(solution)/shard_map/ppermute | solution.py:29
  50.7 7.3 %collective-permute-start.28 = (bf16[64,2048]{1,0:T(8,128)(2,1)S(1)}, bf16[64,2048]{1,0:T(8,128)(2,1)S(1)}, u32[]{:S(2)}, u32[]{:S(2)}) collective-permute-start(bf16[64,2048]{1,0:T(8,128)(2,1)S(1)} %collective-permute-done.20.refs_19_), channel_id=1, source_target_pairs={{0,16},{1,113},{2,18},{3,115},{4,20},{5,117},{6,22},{7,119},{8,120... | collective-permute-start | bytes 786440 | tf_op jit(solution)/shard_map/ppermute | solution.py:29
  52.6 7.9 %collective-permute-start.30 = (bf16[64,2048]{1,0:T(8,128)(2,1)S(1)}, bf16[64,2048]{1,0:T(8,128)(2,1)}, u32[]{:S(2)}, u32[]{:S(2)}) collective-permute-start(bf16[64,2048]{1,0:T(8,128)(2,1)S(1)} %collective-permute-done.20.refs_19_), channel_id=1, source_target_pairs={{0,3},{1,0},{2,1},{3,2},{4,7},{5,4},{6,5},{7,6},{8,9},{9,10},{10,1... | collective-permute-start | bytes 786440 | tf_op jit(solution)/shard_map/ppermute | solution.py:29
  54.7 11.7 %collective-permute-start.24 = (bf16[64,2048]{1,0:T(8,128)(2,1)S(1)}, bf16[64,2048]{1,0:T(8,128)(2,1)}, u32[]{:S(2)}, u32[]{:S(2)}) collective-permute-start(bf16[64,2048]{1,0:T(8,128)(2,1)S(1)} %collective-permute-done.20.refs_19_), channel_id=1, source_target_pairs={{0,8},{1,9},{2,10},{3,11},{4,12},{5,13},{6,14},{7,15},{8,0},{9,1},... | collective-permute-start | bytes 786440 | tf_op jit(solution)/shard_map/ppermute | solution.py:29
  57.1 10.2 %collective-permute-start.27 = (bf16[64,2048]{1,0:T(8,128)(2,1)S(1)}, bf16[64,2048]{1,0:T(8,128)(2,1)}, u32[]{:S(2)}, u32[]{:S(2)}) collective-permute-start(bf16[64,2048]{1,0:T(8,128)(2,1)S(1)} %collective-permute-done.19.refs_18_), channel_id=1, source_target_pairs={{0,16},{1,113},{2,18},{3,115},{4,20},{5,117},{6,22},{7,119},{8,120... | collective-permute-start | bytes 786440 | tf_op jit(solution)/shard_map/ppermute | solution.py:29
  58.0 9.7 %collective-permute-start.29 = (bf16[64,2048]{1,0:T(8,128)(2,1)S(1)}, bf16[64,2048]{1,0:T(8,128)(2,1)}, u32[]{:S(2)}, u32[]{:S(2)}) collective-permute-start(bf16[64,2048]{1,0:T(8,128)(2,1)S(1)} %collective-permute-done.19.refs_18_), channel_id=1, source_target_pairs={{0,3},{1,0},{2,1},{3,2},{4,7},{5,4},{6,5},{7,6},{8,9},{9,10},{10,1... | collective-permute-start | bytes 786440 | tf_op jit(solution)/shard_map/ppermute | solution.py:29
  58.0 9.8 %collective-permute-start.23 = (bf16[64,2048]{1,0:T(8,128)(2,1)S(1)}, bf16[64,2048]{1,0:T(8,128)(2,1)}, u32[]{:S(2)}, u32[]{:S(2)}) collective-permute-start(bf16[64,2048]{1,0:T(8,128)(2,1)S(1)} %collective-permute-done.19.refs_18_), channel_id=1, source_target_pairs={{0,8},{1,9},{2,10},{3,11},{4,12},{5,13},{6,14},{7,15},{8,0},{9,1},... | collective-permute-start | bytes 786440 | tf_op jit(solution)/shard_map/ppermute | solution.py:29
  60.5 6.7 %collective-permute-start.26 = (bf16[64,2048]{1,0:T(8,128)(2,1)S(1)}, bf16[64,2048]{1,0:T(8,128)(2,1)}, u32[]{:S(2)}, u32[]{:S(2)}) collective-permute-start(bf16[64,2048]{1,0:T(8,128)(2,1)S(1)} %collective-permute-done.22.refs_21_), channel_id=1, source_target_pairs={{0,8},{1,9},{2,10},{3,11},{4,12},{5,13},{6,14},{7,15},{8,0},{9,1},... | collective-permute-start | bytes 786440 | tf_op jit(solution)/shard_map/ppermute | solution.py:29
  62.6 14.7 %all-to-all-start = ((bf16[8,8,2048]{2,1,0:T(8,128)(2,1)}), bf16[8,8,2048]{2,1,0:T(8,128)(2,1)S(1)}, u32[]{:S(2)}, u32[]{:S(2)}) async-start(bf16[8,8,2048]{2,1,0:T(8,128)(2,1)} %fusion.102), calls=%async_computation | async-start | bytes 524288 | tf_op jit(solution)/shard_map/all_to_all | solution.py:297
  78.3 2.8 %collective-permute-start.35 = (f32[2,8,128]{2,1,0:T(8,128)S(1)}, f32[2,8,128]{2,1,0:T(8,128)S(1)}, u32[]{:S(2)}, u32[]{:S(2)}) collective-permute-start(f32[2,8,128]{2,1,0:T(8,128)S(1)} %pad_maximum_fusion.3), channel_id=1, source_target_pairs={{0,8},{1,9},{2,10},{3,11},{4,12},{5,13},{6,14},{7,15},{8,0},{9,1},... | collective-permute-start | bytes 24584 | tf_op jit(solution)/shard_map/ppermute | solution.py:29
  81.8 13.1 %all-to-all-start.1 = ((f32[16,2,8,128]{3,2,1,0:T(8,128)}), f32[16,2,8,128]{3,2,1,0:T(8,128)S(1)}, u32[]{:S(2)}, u32[]{:S(2)}) async-start(f32[16,2,8,128]{3,2,1,0:T(8,128)} %broadcast_in_dim.239), calls=%async_computation.1 | async-start | bytes 262144 | tf_op jit(solution)/shard_map/all_to_all | solution.py:60
  95.5 10.9 %all-to-all-start.2 = ((f32[8,2,8,128]{3,2,1,0:T(8,128)}), f32[8,2,8,128]{3,2,1,0:T(8,128)S(1)}, u32[]{:S(2)}, u32[]{:S(2)}) async-start(f32[8,2,8,128]{3,2,1,0:T(8,128)} %broadcast_in_dim.240), calls=%async_computation.2 | async-start | bytes 131072 | tf_op jit(solution)/shard_map/all_to_all | solution.py:60
  106.5 4.2 %collective-permute-start.36 = (f32[2,8,128]{2,1,0:T(8,128)S(1)}, f32[2,8,128]{2,1,0:T(8,128)S(1)}, u32[]{:S(2)}, u32[]{:S(2)}) collective-permute-start(f32[2,8,128]{2,1,0:T(8,128)S(1)} %pad_maximum_fusion.6), channel_id=1, source_target_pairs={{0,8},{1,9},{2,10},{3,11},{4,12},{5,13},{6,14},{7,15},{8,0},{9,1},... | collective-permute-start | bytes 24584 | tf_op jit(solution)/shard_map/ppermute | solution.py:29
  (28 other events, 379.8 us)
where the time goes:
time: 119 us; the launch traced here: 118 us
  starting transfers between devices  61 us (51%)
  waiting for transfers between devices  24.4 us (21%)
  other arithmetic  12.3 us (10%)
  Pallas kernels  11.9 us (10%)
  local copies, waits for them, and re-layouts  6.34 us (5%)
  matrix products  1.26 us (1%)
  between operations  1.19 us (1%)
    ppermute x35, starting transfers between devices, moved(): return lax.ppermute(block, AXES, pairs)  47.4 us
    ppermute x35, waiting for transfers between devices, moved(): return lax.ppermute(block, AXES, pairs)  12.5 us
    all_to_all x2, waiting for transfers between devices, shared(): lax.all_to_all(jnp.broadcast_to(value, (count, *value.shape)), axes, 0, 0...  10.7 us
    all_to_all x2, starting transfers between devices, shared(): lax.all_to_all(jnp.broadcast_to(value, (count, *value.shape)), axes, 0, 0...  9.93 us
    pallas_call x1, Pallas kernels, scored(): pl.pallas_call(lambda *refs: score_kernel(len(parts), refs), out_shape=[j...  6.04 us
    pallas_call x1, Pallas kernels, gradient(): pl.pallas_call(lambda *refs: gradient_kernel(len(scores), len(parts), ref...  5.86 us
    all_to_all x1, starting transfers between devices, whole(): got = lax.all_to_all(sent, 'z', 0, 0, tiled=True)  3.73 us
  transfers between devices with their start and end apart: 38, of which 13 were waited for; matrix products, arithmetic and copies ran while one was open for 12% of the time, Pallas kernels for 5%

commit v1 on v0

--- a/solution.py
+++ b/solution.py
@@ -115,10 +115,11 @@
         value = lax.dot_general(
             table_here[...], rows_here[at, :], (((1,), (1,)), ((), ())), preferred_element_type=jnp.float32
         )
+        peak = jnp.max(value, axis=0, keepdims=True)
+        value = jnp.exp(value - peak)
         scores[:, at] = value
-        peak = jnp.max(value, axis=0, keepdims=True)
         stats[0:1, at] = peak
-        stats[1:2, at] = jnp.sum(jnp.exp(value - peak), axis=0, keepdims=True)
+        stats[1:2, at] = jnp.sum(value, axis=0, keepdims=True)
         return carry
 
     lax.fori_loop(0, rows_here.shape[0] // CHUNK, step, 0)
@@ -147,20 +148,22 @@
     )(start.reshape(1), table, *parts)
 
 
-def gradient_kernel(tables, count, refs):
-    base, peak, total, targets, slots = refs[:5]
-    gots, scores = refs[5:7], refs[7 : 7 + tables]
-    parts = refs[7 + tables : 7 + tables + count]
-    out, scores_here, rows_here, got_here, result, outgoing, sems = refs[7 + tables + count :]
+def gradient_kernel(count, refs):
+    base, factor, targets, slots = refs[:4]
+    gots, scores = refs[4:6], refs[6]
+    parts = refs[7 : 7 + count]
+    out, scores_here, rows_here, got_here, result, outgoing, sems = refs[7 + count :]
     lines, width = out.shape
-    at, views = 0, []
-    for table in scores:
-        views.append(scores_here.at[:, pl.ds(at, table.shape[1])])
-        at += table.shape[1]
-    copies = fetch(
-        [*scores, *gots, *parts], views + stacked(got_here, gots) + stacked(rows_here, parts), sems
-    )
-    for copy in copies[: tables + 2]:
+    tokens, each = rows_here.shape[0], parts[0].shape[0]
+    chunks = tokens // CHUNK
+    sources, views, order = [*gots], stacked(got_here, gots), stacked(rows_here, parts)
+    copies = fetch(sources, views, sems)
+    for k in range(chunks):
+        at = pl.ds(k * CHUNK, CHUNK)
+        pltpu.make_async_copy(scores.at[:, at], scores_here.at[k], sems.at[2 + k]).start()
+        for j in range(k * CHUNK // each, (k + 1) * CHUNK // each):
+            pltpu.make_async_copy(parts[j], order[j], sems.at[2 + chunks + j]).start()
+    for copy in copies:
         copy.wait()
     row = base[0] + lax.broadcasted_iota(jnp.int32, (lines, 1), 0)
     first = jnp.where(row == slots[...], 1.0, 0.0).astype(got_here.dtype)
@@ -168,24 +171,23 @@
     columns = [slice(k * span, (k + 1) * span) for k in range(width // span)]
     for cols in columns:
         result[:, cols] = jnp.dot(first, got_here[:, cols], preferred_element_type=jnp.float32)
-    each = parts[0].shape[0]
 
     def step(k, carry):
-        await_rows(rows_here, each, CHUNK // each, k, sems, tables + 2)
+        pltpu.make_async_copy(scores_here.at[k], scores_here.at[k], sems.at[2 + k]).wait()
+        await_rows(rows_here, each, CHUNK // each, k, sems, 2 + chunks)
         at = pl.ds(pl.multiple_of(k * CHUNK, CHUNK), CHUNK)
         hot = jnp.where(row == targets[:, at], 1.0, 0.0)
-        soft = jnp.exp(scores_here[:, at] - peak[:, at]) * (1.0 / total[:, at])
-        weights = (soft - hot).astype(rows_here.dtype)
+        weights = (scores_here[k] * factor[:, at] - hot).astype(rows_here.dtype)
         for cols in columns:
             result[:, cols] += jnp.dot(weights, rows_here[at, cols], preferred_element_type=jnp.float32)
         return carry
 
-    lax.fori_loop(0, rows_here.shape[0] // CHUNK, step, 0)
+    lax.fori_loop(0, chunks, step, 0)
     stores = []
     for k, cols in enumerate(columns):
         outgoing[k] = result[:, cols].astype(out.dtype)
         store = pltpu.make_async_copy(
-            outgoing.at[k], out.at[:, pl.ds(k * span, span)], sems.at[len(copies) + k]
+            outgoing.at[k], out.at[:, pl.ds(k * span, span)], sems.at[2 + chunks + count + k]
         )
         store.start()
         stores.append(store)
@@ -193,27 +195,27 @@
         store.wait()
 
 
-def gradient(dtype, lines, base, scores, parts, peak, total, targets, slots, gots):
-    tokens, width = peak.shape[1], gots[0].shape[1]
-    step = width // 4
+def gradient(dtype, lines, base, scores, parts, factor, targets, slots, gots):
+    tokens, width = factor.shape[1], gots[0].shape[1]
+    span, chunks = width // 4, tokens // CHUNK
     return pl.pallas_call(
-        lambda *refs: gradient_kernel(len(scores), len(parts), refs),
+        lambda *refs: gradient_kernel(len(parts), refs),
         out_shape=jax.ShapeDtypeStruct((lines, width), dtype),
-        in_specs=[pl.BlockSpec(memory_space=pltpu.SMEM)] + in_vmem(4) + anywhere(2 + len(scores) + len(parts)),
+        in_specs=[pl.BlockSpec(memory_space=pltpu.SMEM)] + in_vmem(3) + anywhere(3 + len(parts)),
         out_specs=pl.BlockSpec(memory_space=pl.ANY),
         scratch_shapes=[
-            pltpu.VMEM((lines, tokens), jnp.float32),
+            pltpu.VMEM((chunks, lines, CHUNK), jnp.float32),
             pltpu.VMEM((tokens, width), jnp.bfloat16),
             pltpu.VMEM((2 * gots[0].shape[0], width), jnp.bfloat16),
             pltpu.VMEM((lines, width), jnp.float32),
-            pltpu.VMEM((width // step, lines, step), dtype),
-            pltpu.SemaphoreType.DMA((2 + len(scores) + len(parts) + width // step,)),
+            pltpu.VMEM((width // span, lines, span), dtype),
+            pltpu.SemaphoreType.DMA((2 + chunks + len(parts) + width // span,)),
         ],
         cost_estimate=pl.CostEstimate(
-            flops=2 * tokens * lines * width, bytes_accessed=2 * width * tokens, transcendentals=lines * tokens
+            flops=2 * tokens * lines * width, bytes_accessed=2 * width * tokens, transcendentals=0
         ),
         name="gradient",
-    )(base.reshape(1), peak, total, targets, slots, *gots, *scores, *parts)
+    )(base.reshape(1), factor, targets, slots, *gots, scores, *parts)
 
 
 def whole(activations, token_ids, embed_table):
@@ -294,12 +296,12 @@
     filled = in_match[:, None, :] & (in_rank[:, None, :] == slot[None, :, None])
     slots = jnp.sum(jnp.where(filled, shard_in[:, None, :] + 1, 0), axis=2).reshape(1, shards * SLOTS) - 1
 
-    got = lax.all_to_all(sent, "z", 0, 0, tiled=True)
-
     there, back = [[block] for block in blocks], [[] for _ in blocks]
     for step in range(1, nz // 2 + 1):
         for k in range(SUBS):
             block = there[k][-1]
+            if step == 3 and k == 0:
+                block, slots, targets, sent = lax.optimization_barrier((block, slots, targets, sent))
             there[k].append(moved(block, along_z))
             if step > 1:
                 back[k].append(moved(block, along_x))
@@ -309,9 +311,10 @@
         for hop in hops[pair : pair + 2]:
             group += [there[k][hop] if hop >= 0 else back[k][-hop - 1] for k in range(SUBS)]
         parts += group + [moved(p, other_core) for p in group]
+    got = lax.all_to_all(sent, "z", 0, 0, tiled=True)
     table_scores, stats = scored(s * half, half, embed_table, parts)
     stats, got = lax.optimization_barrier((stats, got))
-    scores = [table_scores]
+    scores = table_scores
     gots = (got, moved(got, other_core))
 
     local = stats.reshape(2, shards, rows)
@@ -323,8 +326,8 @@
     pair = joined(shared(pair, ("s", "u", "x")))
     pair = joined(shared(pair, "z"))
     pair = jnp.concatenate([pair, moved(pair, other_core)], axis=1)
-    peak_all = picked(pair[0], order).reshape(1, shards * rows)
-    total_all = picked(pair[1], order).reshape(1, shards * rows)
+    factor = jnp.exp(local[0] - picked(pair[0], order)) / picked(pair[1], order)
+    factor = factor.reshape(1, shards * rows)
 
     def plain(cot, token_ids, args):
         return gradient(jnp.bfloat16, half, *args)
@@ -353,7 +356,7 @@
         total, _ = lax.fori_loop(0, nz, step, (gradient(jnp.float32, half, *args), cot))
         return total.astype(jnp.bfloat16)
 
-    args = (base, scores, parts, peak_all, total_all, targets, slots, gots)
+    args = (base, scores, parts, factor, targets, slots, gots)
     out = lax.cond(crowded, crowded_too, plain, cot, token_ids, args)
     return out.reshape(1, 1, half, width)
 

time: 119 us -> 114 us (0.958)
  blocking collectives: 0 us -> 24.4 us
  starting transfers between devices: 61 us -> 48.7 us
  waiting for transfers between devices: 24.4 us -> 16.9 us
  other arithmetic: 12.3 us -> 5.66 us
  local copies, waits for them, and re-layouts: 6.34 us -> 3.68 us
    all_to_all x0 -> x2, blocking collectives: none -> 24.4 us  [shared(): lax.all_to_all(jnp.broadcast_to(value, (count, *value.shape)), axes, 0, 0...]
    all_to_all x2 -> x0, waiting for transfers between devices: 10.7 us -> none  [shared(): lax.all_to_all(jnp.broadcast_to(value, (count, *value.shape)), axes, 0, 0...]
    all_to_all x2 -> x0, starting transfers between devices: 9.93 us -> none  [shared(): lax.all_to_all(jnp.broadcast_to(value, (count, *value.shape)), axes, 0, 0...]
    ppermute x35, starting transfers between devices: 47.4 us -> 45.3 us  [moved(): return lax.ppermute(block, AXES, pairs)]
    ppermute x35, waiting for transfers between devices: 12.5 us -> 14.3 us  [moved(): return lax.ppermute(block, AXES, pairs)]
    reduce_sum x4, other arithmetic: 1.82 us -> 0.45 us  [picked(): jnp.sum(jnp.where(hit, table[None], jnp.zeros((), table.dtype)), axis=1)]
    all_to_all x1, waiting for transfers between devices: 1.22 us -> 2.59 us  [whole(): got = lax.all_to_all(sent, 'z', 0, 0, tiled=True)]
    broadcast_in_dim x2, local copies, waits for them, and re-layouts: 1.3 us -> 0.02 us  [shared(): jnp.broadcast_to(value, (count, *value.shape))]
  transfers between devices with their start and end apart: 38 -> 36, of which waited for: 13 -> 14; matrix products, arithmetic and copies ran while one was open for 12% -> 7% of each run, Pallas kernels for 5% -> 5%
where the time goes in v1:
time: 114 us
  starting transfers between devices  48.7 us (43%)
  blocking collectives  24.4 us (21%)
  waiting for transfers between devices  16.9 us (15%)
  Pallas kernels  11.9 us (10%)
  other arithmetic  5.66 us (5%)
  local copies, waits for them, and re-layouts  3.68 us (3%)
  between operations  1.33 us (1%)
  matrix products  1.26 us (1%)
    ppermute x35, starting transfers between devices, moved(): return lax.ppermute(block, AXES, pairs)  45.3 us
    all_to_all x2, blocking collectives, shared(): lax.all_to_all(jnp.broadcast_to(value, (count, *value.shape)), axes, 0, 0...  24.4 us
    ppermute x35, waiting for transfers between devices, moved(): return lax.ppermute(block, AXES, pairs)  14.3 us
    pallas_call x1, Pallas kernels, scored(): pl.pallas_call(lambda *refs: score_kernel(len(parts), refs), out_shape=[j...  6.08 us
    pallas_call x1, Pallas kernels, gradient(): pl.pallas_call(lambda *refs: gradient_kernel(len(parts), refs), out_shape...  5.81 us
    all_to_all x1, starting transfers between devices, whole(): got = lax.all_to_all(sent, 'z', 0, 0, tiled=True)  3.42 us
    all_to_all x1, waiting for transfers between devices, whole(): got = lax.all_to_all(sent, 'z', 0, 0, tiled=True)  2.59 us
  transfers between devices with their start and end apart: 36, of which 14 were waited for; matrix products, arithmetic and copies ran while one was open for 7% of the time, Pallas kernels for 5%

profile of v1, /device:TPU:1, one launch (start us, length us, event | category | flops | bytes accessed | tf_op | source)
XLA Modules:
  0.0 113.8 jit_solution(8020332862769975128)
XLA Ops:
  0.0 1.1 slice_bitcast_fusion.1
  1.1 3.6 %collective-permute-start.3 = (bf16[64,2048]{1,0:T(8,128)(2,1)S(1)}, bf16[64,2048]{1,0:T(8,128)(2,1)S(1)}, u32[]{:S(2)}, u32[]{:S(2)}) collective-permute-start(bf16[64,2048]{1,0:T(8,128)(2,1)S(1)} %get-tuple-element.683), channel_id=1, source_target_pairs={{0,132},{1,133},{2,134},{3,135},{4,128},{5,129},{6,130},{7,131},{8... | collective-permute-start | bytes 786440 | tf_op jit(solution)/shard_map/ppermute | solution.py:29
  4.9 0.8 fusion.166
  8.5 1.3 %collective-permute-done.3 = bf16[64,2048]{1,0:T(8,128)(2,1)S(1)} collective-permute-done((bf16[64,2048]{1,0:T(8,128)(2,1)S(1)}, bf16[64,2048]{1,0:T(8,128)(2,1)S(1)}, u32[]{:S(2)}, u32[]{:S(2)}) %collective-permute-start.3) | collective-permute-done | bytes 262176 | tf_op jit(solution)/shard_map/ppermute | solution.py:29
  9.8 1.0 broadcast_select_fusion.3
  10.7 4.6 %collective-permute-done.4 = bf16[64,2048]{1,0:T(8,128)(2,1)S(1)} collective-permute-done((bf16[64,2048]{1,0:T(8,128)(2,1)S(1)}, bf16[64,2048]{1,0:T(8,128)(2,1)S(1)}, u32[]{:S(2)}, u32[]{:S(2)}) %collective-permute-start.4) | collective-permute-done | bytes 262176 | tf_op jit(solution)/shard_map/ppermute | solution.py:29
  15.4 6.4 %collective-permute-start.5 = (bf16[64,2048]{1,0:T(8,128)(2,1)S(1)}, bf16[64,2048]{1,0:T(8,128)(2,1)S(1)}, u32[]{:S(2)}, u32[]{:S(2)}) collective-permute-start(bf16[64,2048]{1,0:T(8,128)(2,1)S(1)} %get-tuple-element.603.refs_2_), channel_id=1, source_target_pairs={{0,16},{1,113},{2,18},{3,115},{4,20},{5,117},{6,22},{7,119},{8,120... | collective-permute-start | bytes 786440 | tf_op jit(solution)/shard_map/ppermute | solution.py:29
  21.8 0.8 collective-permute-start.6
  23.1 2.0 %collective-permute-done.5.refs_4_ = bf16[64,2048]{1,0:T(8,128)(2,1)S(1)} collective-permute-done((bf16[64,2048]{1,0:T(8,128)(2,1)S(1)}, bf16[64,2048]{1,0:T(8,128)(2,1)S(1)}, u32[]{:S(2)}, u32[]{:S(2)}) %collective-permute-start.5) | collective-permute-done | bytes 262176 | tf_op jit(solution)/shard_map/ppermute | solution.py:29
  25.1 3.1 %collective-permute-start.11 = (bf16[64,2048]{1,0:T(8,128)(2,1)S(1)}, bf16[64,2048]{1,0:T(8,128)(2,1)S(1)}, u32[]{:S(2)}, u32[]{:S(2)}) collective-permute-start(bf16[64,2048]{1,0:T(8,128)(2,1)S(1)} %collective-permute-done.5.refs_4_), channel_id=1, source_target_pairs={{0,16},{1,113},{2,18},{3,115},{4,20},{5,117},{6,22},{7,119},{8,120... | collective-permute-start | bytes 786440 | tf_op jit(solution)/shard_map/ppermute | solution.py:29
  29.9 1.1 collective-permute-start.12
  31.0 5.7 %collective-permute-start.10 = (bf16[64,2048]{1,0:T(8,128)(2,1)S(1)}, bf16[64,2048]{1,0:T(8,128)(2,1)S(1)}, u32[]{:S(2)}, u32[]{:S(2)}) collective-permute-start(bf16[64,2048]{1,0:T(8,128)(2,1)S(1)} %collective-permute-done.6.refs_5_), channel_id=1, source_target_pairs={{0,8},{1,9},{2,10},{3,11},{4,12},{5,13},{6,14},{7,15},{8,0},{9,1},... | collective-permute-start | bytes 786440 | tf_op jit(solution)/shard_map/ppermute | solution.py:29
  37.4 1.0 convolution_convert_fusion
  38.5 1.8 %collective-permute-start.21 = (bf16[64,2048]{1,0:T(8,128)(2,1)S(1)}, bf16[64,2048]{1,0:T(8,128)(2,1)S(1)}, u32[]{:S(2)}, u32[]{:S(2)}) collective-permute-start(bf16[64,2048]{1,0:T(8,128)(2,1)S(1)} %collective-permute-done.11.refs_10_), channel_id=1, source_target_pairs={{0,3},{1,0},{2,1},{3,2},{4,7},{5,4},{6,5},{7,6},{8,9},{9,10},{10,1... | collective-permute-start | bytes 786440 | tf_op jit(solution)/shard_map/ppermute | solution.py:29
  40.2 2.0 %collective-permute-start.20 = (bf16[64,2048]{1,0:T(8,128)(2,1)S(1)}, bf16[64,2048]{1,0:T(8,128)(2,1)S(1)}, u32[]{:S(2)}, u32[]{:S(2)}) collective-permute-start(bf16[64,2048]{1,0:T(8,128)(2,1)S(1)} %collective-permute-done.12.refs_11_), channel_id=1, source_target_pairs={{0,16},{1,113},{2,18},{3,115},{4,20},{5,117},{6,22},{7,119},{8,120... | collective-permute-start | bytes 786440 | tf_op jit(solution)/shard_map/ppermute | solution.py:29
  42.2 1.1 %collective-permute-done.13.refs_12_ = bf16[64,2048]{1,0:T(8,128)(2,1)S(1)} collective-permute-done((bf16[64,2048]{1,0:T(8,128)(2,1)S(1)}, bf16[64,2048]{1,0:T(8,128)(2,1)S(1)}, u32[]{:S(2)}, u32[]{:S(2)}) %collective-permute-start.13) | collective-permute-done | bytes 262176 | tf_op jit(solution)/shard_map/ppermute | solution.py:29
  43.4 3.6 %collective-permute-start.16 = (bf16[64,2048]{1,0:T(8,128)(2,1)S(1)}, bf16[64,2048]{1,0:T(8,128)(2,1)S(1)}, u32[]{:S(2)}, u32[]{:S(2)}) collective-permute-start(bf16[64,2048]{1,0:T(8,128)(2,1)S(1)} %collective-permute-done.12.refs_11_), channel_id=1, source_target_pairs={{0,8},{1,9},{2,10},{3,11},{4,12},{5,13},{6,14},{7,15},{8,0},{9,1},... | collective-permute-start | bytes 786440 | tf_op jit(solution)/shard_map/ppermute | solution.py:29
  47.2 1.0 collective-permute-start.15
  48.1 3.7 %collective-permute-start.17 = (bf16[64,2048]{1,0:T(8,128)(2,1)S(1)}, bf16[64,2048]{1,0:T(8,128)(2,1)S(1)}, u32[]{:S(2)}, u32[]{:S(2)}) collective-permute-start(bf16[64,2048]{1,0:T(8,128)(2,1)S(1)} %collective-permute-done.13.refs_12_), channel_id=1, source_target_pairs={{0,8},{1,9},{2,10},{3,11},{4,12},{5,13},{6,14},{7,15},{8,0},{9,1},... | collective-permute-start | bytes 786440 | tf_op jit(solution)/shard_map/ppermute | solution.py:29
  52.0 3.1 %collective-permute-start.23 = (bf16[64,2048]{1,0:T(8,128)(2,1)S(1)}, bf16[64,2048]{1,0:T(8,128)(2,1)}, u32[]{:S(2)}, u32[]{:S(2)}) collective-permute-start(bf16[64,2048]{1,0:T(8,128)(2,1)S(1)} %collective-permute-done.19.refs_18_), channel_id=1, source_target_pairs={{0,8},{1,9},{2,10},{3,11},{4,12},{5,13},{6,14},{7,15},{8,0},{9,1},... | collective-permute-start | bytes 786440 | tf_op jit(solution)/shard_map/ppermute | solution.py:29
  55.4 2.0 %collective-permute-done.27.refs_26_ = bf16[64,2048]{1,0:T(8,128)(2,1)S(1)} collective-permute-done((bf16[64,2048]{1,0:T(8,128)(2,1)S(1)}, bf16[64,2048]{1,0:T(8,128)(2,1)S(1)}, u32[]{:S(2)}, u32[]{:S(2)}) %collective-permute-start.27) | collective-permute-done | bytes 262176 | tf_op jit(solution)/shard_map/ppermute | solution.py:29
  57.4 2.2 %collective-permute-start.24 = (bf16[64,2048]{1,0:T(8,128)(2,1)S(1)}, bf16[64,2048]{1,0:T(8,128)(2,1)}, u32[]{:S(2)}, u32[]{:S(2)}) collective-permute-start(bf16[64,2048]{1,0:T(8,128)(2,1)S(1)} %collective-permute-done.20.refs_19_), channel_id=1, source_target_pairs={{0,8},{1,9},{2,10},{3,11},{4,12},{5,13},{6,14},{7,15},{8,0},{9,1},... | collective-permute-start | bytes 786440 | tf_op jit(solution)/shard_map/ppermute | solution.py:29
  59.9 3.4 %all-to-all-start = ((bf16[8,8,2048]{2,1,0:T(8,128)(2,1)}), bf16[8,8,2048]{2,1,0:T(8,128)(2,1)S(1)}, u32[]{:S(2)}, u32[]{:S(2)}) async-start(bf16[8,8,2048]{2,1,0:T(8,128)(2,1)} %bitcast.233), calls=%async_computation | async-start | bytes 524288 | tf_op jit(solution)/shard_map/all_to_all | solution.py:314
  66.7 6.1 %score.1 = (f32[256,2048]{1,0:T(8,128)S(1)}, f32[2,2048]{1,0:T(2,128)}) custom-call(s32[1]{0:T(128)} %bitcast.7.refs_0_, bf16[512,2048]{1,0:T(8,128)(2,1)} %refs_1_.1, bf16[64,2048]{1,0:T(8,128)(2,1)S(1)} %get-tuple-element.603.refs_2_, bf16[64,2048]{1,0:T(8,128)(2,1)S(1)} %get-tuple-element.679.refs_3_, bf16[64,2048]{1,0:T(8,128)(2,1)} %copy-done.1, ...), custom_call_target="tpu_custom_call" | custom-call | flops 2147483648 | bytes 9437184 | tf_op jit(solution)/shard_map/score/pallas_call | solution.py:131
  72.8 2.6 %all-to-all-done = bf16[8,8,2048]{2,1,0:T(8,128)(2,1)S(1)} async-done(((bf16[8,8,2048]{2,1,0:T(8,128)(2,1)}), bf16[8,8,2048]{2,1,0:T(8,128)(2,1)S(1)}, u32[]{:S(2)}, u32[]{:S(2)}) %all-to-all-start) | async-done | bytes 262176 | tf_op jit(solution)/shard_map/all_to_all | solution.py:314
  75.4 0.8 fusion.165
  77.1 0.8 collective-permute-done.35
  78.0 13.6 %all_to_all.22 = f32[16,2,8,128]{3,2,1,0:T(8,128)S(1)} all-to-all(f32[16,2,8,128]{3,2,1,0:T(8,128)S(1)} %broadcast_in_dim.244), channel_id=1, replica_groups=mesh['s'=2,'z'=8,'c'=2,'u'=2,'x'=4] {'s','u','x'}, dimensions={0} | all-to-all | bytes 262144 | tf_op jit(solution)/shard_map/all_to_all | solution.py:60
  91.7 10.8 %all_to_all.23 = f32[8,2,8,128]{3,2,1,0:T(8,128)S(1)} all-to-all(f32[8,2,8,128]{3,2,1,0:T(8,128)S(1)} %broadcast_in_dim.245), channel_id=1, replica_groups=mesh['s'=2,'z'=8,'c'=2,'u'=2,'x'=4] {'z'}, dimensions={0} | all-to-all | bytes 131072 | tf_op jit(solution)/shard_map/all_to_all | solution.py:60
  102.5 3.5 %collective-permute-start.36 = (f32[2,8,128]{2,1,0:T(8,128)S(1)}, f32[2,8,128]{2,1,0:T(8,128)S(1)}, u32[]{:S(2)}, u32[]{:S(2)}) collective-permute-start(f32[2,8,128]{2,1,0:T(8,128)S(1)} %pad_maximum_fusion.6), channel_id=1, source_target_pairs={{0,8},{1,9},{2,10},{3,11},{4,12},{5,13},{6,14},{7,15},{8,0},{9,1},... | collective-permute-start | bytes 24584 | tf_op jit(solution)/shard_map/ppermute | solution.py:29
  107.8 5.8 %conditional.1 = (bf16[1,1,256,2048]{3,2,1,0:T(8,128)(2,1)}) conditional(s32[]{:T(128)} %convert_element_type.63, (s32[]{:T(128)}, f32[1,2048]{1,0:T(1,128)S(1)}, s32[1,2048]{1,0:T(1,128)S(1)}, s32[1,128]{1,0:T(1,128)S(1)}, bf16[64,2048]{1,0:T(8,128)(2,1)S(1)}, /*index=5*/bf16[64,2048]{1,0:T(8,128)(2,1)}, f32[256,2048]{1,0:T(8,128)S(1)}, ...), branch_computations={%region_22.23_spmd, %region_23.26_spmd} | conditional | flops 2417656064 | bytes 35751588 | solution.py:360
  107.8 5.8 %gradient.2 = bf16[256,2048]{1,0:T(8,128)(2,1)} custom-call(s32[1]{0:T(128)} %bitcast.refs_0_, f32[1,2048]{1,0:T(1,128)S(1)} %get-tuple-element.490.refs_1_, s32[1,2048]{1,0:T(1,128)S(1)} %get-tuple-element.491.refs_2_, s32[1,128]{1,0:T(1,128)S(1)} %get-tuple-element.492.refs_3_, bf16[64,2048]{1,0:T(8,128)(2,1)S(1)} %get-tuple-element.493.refs_4_, ...), custom_call_target="tpu_custom_call" | custom-call | flops 2147483648 | bytes 8388608 | tf_op jit(solution)/shard_map/cond/branch_0_fun/gradient/pallas_call | solution.py:201
  (145 shorter events, 12.1 us)
Async XLA Ops:
  1.1 8.6 %collective-permute-start.3 = (bf16[64,2048]{1,0:T(8,128)(2,1)S(1)}, bf16[64,2048]{1,0:T(8,128)(2,1)S(1)}, u32[]{:S(2)}, u32[]{:S(2)}) collective-permute-start(bf16[64,2048]{1,0:T(8,128)(2,1)S(1)} %get-tuple-element.683), channel_id=1, source_target_pairs={{0,132},{1,133},{2,134},{3,135},{4,128},{5,129},{6,130},{7,131},{8... | collective-permute-start | bytes 786440 | tf_op jit(solution)/shard_map/ppermute | solution.py:29
  4.8 10.6 %collective-permute-start.4 = (bf16[64,2048]{1,0:T(8,128)(2,1)S(1)}, bf16[64,2048]{1,0:T(8,128)(2,1)S(1)}, u32[]{:S(2)}, u32[]{:S(2)}) collective-permute-start(bf16[64,2048]{1,0:T(8,128)(2,1)S(1)} %get-tuple-element.684), channel_id=1, source_target_pairs={{0,132},{1,133},{2,134},{3,135},{4,128},{5,129},{6,130},{7,131},{8... | collective-permute-start | bytes 786440 | tf_op jit(solution)/shard_map/ppermute | solution.py:29
  15.4 9.7 %collective-permute-start.5 = (bf16[64,2048]{1,0:T(8,128)(2,1)S(1)}, bf16[64,2048]{1,0:T(8,128)(2,1)S(1)}, u32[]{:S(2)}, u32[]{:S(2)}) collective-permute-start(bf16[64,2048]{1,0:T(8,128)(2,1)S(1)} %get-tuple-element.603.refs_2_), channel_id=1, source_target_pairs={{0,16},{1,113},{2,18},{3,115},{4,20},{5,117},{6,22},{7,119},{8,120... | collective-permute-start | bytes 786440 | tf_op jit(solution)/shard_map/ppermute | solution.py:29
  21.8 8.1 %collective-permute-start.6 = (bf16[64,2048]{1,0:T(8,128)(2,1)S(1)}, bf16[64,2048]{1,0:T(8,128)(2,1)S(1)}, u32[]{:S(2)}, u32[]{:S(2)}) collective-permute-start(bf16[64,2048]{1,0:T(8,128)(2,1)S(1)} %get-tuple-element.679.refs_3_), channel_id=1, source_target_pairs={{0,16},{1,113},{2,18},{3,115},{4,20},{5,117},{6,22},{7,119},{8,120... | collective-permute-start | bytes 786440 | tf_op jit(solution)/shard_map/ppermute | solution.py:29
  22.6 8.4 %collective-permute-start.8 = (bf16[64,2048]{1,0:T(8,128)(2,1)S(1)}, bf16[64,2048]{1,0:T(8,128)(2,1)S(1)}, u32[]{:S(2)}, u32[]{:S(2)}) collective-permute-start(bf16[64,2048]{1,0:T(8,128)(2,1)S(1)} %get-tuple-element.679.refs_3_), channel_id=1, source_target_pairs={{0,8},{1,9},{2,10},{3,11},{4,12},{5,13},{6,14},{7,15},{8,0},{9,1},... | collective-permute-start | bytes 786440 | tf_op jit(solution)/shard_map/ppermute | solution.py:29
  22.6 14.1 %collective-permute-start.7 = (bf16[64,2048]{1,0:T(8,128)(2,1)S(1)}, bf16[64,2048]{1,0:T(8,128)(2,1)S(1)}, u32[]{:S(2)}, u32[]{:S(2)}) collective-permute-start(bf16[64,2048]{1,0:T(8,128)(2,1)S(1)} %get-tuple-element.603.refs_2_), channel_id=1, source_target_pairs={{0,8},{1,9},{2,10},{3,11},{4,12},{5,13},{6,14},{7,15},{8,0},{9,1},... | collective-permute-start | bytes 786440 | tf_op jit(solution)/shard_map/ppermute | solution.py:29
  25.1 11.6 %collective-permute-start.11 = (bf16[64,2048]{1,0:T(8,128)(2,1)S(1)}, bf16[64,2048]{1,0:T(8,128)(2,1)S(1)}, u32[]{:S(2)}, u32[]{:S(2)}) collective-permute-start(bf16[64,2048]{1,0:T(8,128)(2,1)S(1)} %collective-permute-done.5.refs_4_), channel_id=1, source_target_pairs={{0,16},{1,113},{2,18},{3,115},{4,20},{5,117},{6,22},{7,119},{8,120... | collective-permute-start | bytes 786440 | tf_op jit(solution)/shard_map/ppermute | solution.py:29
  29.9 8.5 %collective-permute-start.12 = (bf16[64,2048]{1,0:T(8,128)(2,1)S(1)}, bf16[64,2048]{1,0:T(8,128)(2,1)S(1)}, u32[]{:S(2)}, u32[]{:S(2)}) collective-permute-start(bf16[64,2048]{1,0:T(8,128)(2,1)S(1)} %collective-permute-done.6.refs_5_), channel_id=1, source_target_pairs={{0,16},{1,113},{2,18},{3,115},{4,20},{5,117},{6,22},{7,119},{8,120... | collective-permute-start | bytes 786440 | tf_op jit(solution)/shard_map/ppermute | solution.py:29
  31.0 7.4 %collective-permute-start.14 = (bf16[64,2048]{1,0:T(8,128)(2,1)S(1)}, bf16[64,2048]{1,0:T(8,128)(2,1)S(1)}, u32[]{:S(2)}, u32[]{:S(2)}) collective-permute-start(bf16[64,2048]{1,0:T(8,128)(2,1)S(1)} %collective-permute-done.6.refs_5_), channel_id=1, source_target_pairs={{0,3},{1,0},{2,1},{3,2},{4,7},{5,4},{6,5},{7,6},{8,9},{9,10},{10,1... | collective-permute-start | bytes 786440 | tf_op jit(solution)/shard_map/ppermute | solution.py:29
  31.0 9.2 %collective-permute-start.10 = (bf16[64,2048]{1,0:T(8,128)(2,1)S(1)}, bf16[64,2048]{1,0:T(8,128)(2,1)S(1)}, u32[]{:S(2)}, u32[]{:S(2)}) collective-permute-start(bf16[64,2048]{1,0:T(8,128)(2,1)S(1)} %collective-permute-done.6.refs_5_), channel_id=1, source_target_pairs={{0,8},{1,9},{2,10},{3,11},{4,12},{5,13},{6,14},{7,15},{8,0},{9,1},... | collective-permute-start | bytes 786440 | tf_op jit(solution)/shard_map/ppermute | solution.py:29
  36.7 6.7 %collective-permute-start.13 = (bf16[64,2048]{1,0:T(8,128)(2,1)S(1)}, bf16[64,2048]{1,0:T(8,128)(2,1)S(1)}, u32[]{:S(2)}, u32[]{:S(2)}) collective-permute-start(bf16[64,2048]{1,0:T(8,128)(2,1)S(1)} %collective-permute-done.5.refs_4_), channel_id=1, source_target_pairs={{0,3},{1,0},{2,1},{3,2},{4,7},{5,4},{6,5},{7,6},{8,9},{9,10},{10,1... | collective-permute-start | bytes 786440 | tf_op jit(solution)/shard_map/ppermute | solution.py:29
  36.7 6.7 %collective-permute-start.9 = (bf16[64,2048]{1,0:T(8,128)(2,1)S(1)}, bf16[64,2048]{1,0:T(8,128)(2,1)S(1)}, u32[]{:S(2)}, u32[]{:S(2)}) collective-permute-start(bf16[64,2048]{1,0:T(8,128)(2,1)S(1)} %collective-permute-done.5.refs_4_), channel_id=1, source_target_pairs={{0,8},{1,9},{2,10},{3,11},{4,12},{5,13},{6,14},{7,15},{8,0},{9,1},... | collective-permute-start | bytes 786440 | tf_op jit(solution)/shard_map/ppermute | solution.py:29
  38.4 8.6 %collective-permute-start.19 = (bf16[64,2048]{1,0:T(8,128)(2,1)S(1)}, bf16[64,2048]{1,0:T(8,128)(2,1)S(1)}, u32[]{:S(2)}, u32[]{:S(2)}) collective-permute-start(bf16[64,2048]{1,0:T(8,128)(2,1)S(1)} %collective-permute-done.11.refs_10_), channel_id=1, source_target_pairs={{0,16},{1,113},{2,18},{3,115},{4,20},{5,117},{6,22},{7,119},{8,120... | collective-permute-start | bytes 786440 | tf_op jit(solution)/shard_map/ppermute | solution.py:29
  38.5 8.7 %collective-permute-start.21 = (bf16[64,2048]{1,0:T(8,128)(2,1)S(1)}, bf16[64,2048]{1,0:T(8,128)(2,1)S(1)}, u32[]{:S(2)}, u32[]{:S(2)}) collective-permute-start(bf16[64,2048]{1,0:T(8,128)(2,1)S(1)} %collective-permute-done.11.refs_10_), channel_id=1, source_target_pairs={{0,3},{1,0},{2,1},{3,2},{4,7},{5,4},{6,5},{7,6},{8,9},{9,10},{10,1... | collective-permute-start | bytes 786440 | tf_op jit(solution)/shard_map/ppermute | solution.py:29
  40.2 7.9 %collective-permute-start.20 = (bf16[64,2048]{1,0:T(8,128)(2,1)S(1)}, bf16[64,2048]{1,0:T(8,128)(2,1)S(1)}, u32[]{:S(2)}, u32[]{:S(2)}) collective-permute-start(bf16[64,2048]{1,0:T(8,128)(2,1)S(1)} %collective-permute-done.12.refs_11_), channel_id=1, source_target_pairs={{0,16},{1,113},{2,18},{3,115},{4,20},{5,117},{6,22},{7,119},{8,120... | collective-permute-start | bytes 786440 | tf_op jit(solution)/shard_map/ppermute | solution.py:29
  43.4 8.4 %collective-permute-start.22 = (bf16[64,2048]{1,0:T(8,128)(2,1)S(1)}, bf16[64,2048]{1,0:T(8,128)(2,1)S(1)}, u32[]{:S(2)}, u32[]{:S(2)}) collective-permute-start(bf16[64,2048]{1,0:T(8,128)(2,1)S(1)} %collective-permute-done.12.refs_11_), channel_id=1, source_target_pairs={{0,3},{1,0},{2,1},{3,2},{4,7},{5,4},{6,5},{7,6},{8,9},{9,10},{10,1... | collective-permute-start | bytes 786440 | tf_op jit(solution)/shard_map/ppermute | solution.py:29
  43.4 8.4 %collective-permute-start.16 = (bf16[64,2048]{1,0:T(8,128)(2,1)S(1)}, bf16[64,2048]{1,0:T(8,128)(2,1)S(1)}, u32[]{:S(2)}, u32[]{:S(2)}) collective-permute-start(bf16[64,2048]{1,0:T(8,128)(2,1)S(1)} %collective-permute-done.12.refs_11_), channel_id=1, source_target_pairs={{0,8},{1,9},{2,10},{3,11},{4,12},{5,13},{6,14},{7,15},{8,0},{9,1},... | collective-permute-start | bytes 786440 | tf_op jit(solution)/shard_map/ppermute | solution.py:29
  47.1 4.9 %collective-permute-start.18 = (bf16[64,2048]{1,0:T(8,128)(2,1)S(1)}, bf16[64,2048]{1,0:T(8,128)(2,1)S(1)}, u32[]{:S(2)}, u32[]{:S(2)}) collective-permute-start(bf16[64,2048]{1,0:T(8,128)(2,1)S(1)} %collective-permute-done.14.refs_13_), channel_id=1, source_target_pairs={{0,8},{1,9},{2,10},{3,11},{4,12},{5,13},{6,14},{7,15},{8,0},{9,1},... | collective-permute-start | bytes 786440 | tf_op jit(solution)/shard_map/ppermute | solution.py:29
  47.2 7.9 %collective-permute-start.15 = (bf16[64,2048]{1,0:T(8,128)(2,1)S(1)}, bf16[64,2048]{1,0:T(8,128)(2,1)S(1)}, u32[]{:S(2)}, u32[]{:S(2)}) collective-permute-start(bf16[64,2048]{1,0:T(8,128)(2,1)S(1)} %collective-permute-done.11.refs_10_), channel_id=1, source_target_pairs={{0,8},{1,9},{2,10},{3,11},{4,12},{5,13},{6,14},{7,15},{8,0},{9,1},... | collective-permute-start | bytes 786440 | tf_op jit(solution)/shard_map/ppermute | solution.py:29
  48.1 7.1 %collective-permute-start.17 = (bf16[64,2048]{1,0:T(8,128)(2,1)S(1)}, bf16[64,2048]{1,0:T(8,128)(2,1)S(1)}, u32[]{:S(2)}, u32[]{:S(2)}) collective-permute-start(bf16[64,2048]{1,0:T(8,128)(2,1)S(1)} %collective-permute-done.13.refs_12_), channel_id=1, source_target_pairs={{0,8},{1,9},{2,10},{3,11},{4,12},{5,13},{6,14},{7,15},{8,0},{9,1},... | collective-permute-start | bytes 786440 | tf_op jit(solution)/shard_map/ppermute | solution.py:29
  51.8 5.5 %collective-permute-start.27 = (bf16[64,2048]{1,0:T(8,128)(2,1)S(1)}, bf16[64,2048]{1,0:T(8,128)(2,1)S(1)}, u32[]{:S(2)}, u32[]{:S(2)}) collective-permute-start(bf16[64,2048]{1,0:T(8,128)(2,1)S(1)} %collective-permute-done.19.refs_18_), channel_id=1, source_target_pairs={{0,16},{1,113},{2,18},{3,115},{4,20},{5,117},{6,22},{7,119},{8,120... | collective-permute-start | bytes 786440 | tf_op jit(solution)/shard_map/ppermute | solution.py:29
  51.9 7.7 %collective-permute-start.29 = (bf16[64,2048]{1,0:T(8,128)(2,1)S(1)}, bf16[64,2048]{1,0:T(8,128)(2,1)S(1)}, u32[]{:S(2)}, u32[]{:S(2)}) collective-permute-start(bf16[64,2048]{1,0:T(8,128)(2,1)S(1)} %collective-permute-done.19.refs_18_), channel_id=1, source_target_pairs={{0,3},{1,0},{2,1},{3,2},{4,7},{5,4},{6,5},{7,6},{8,9},{9,10},{10,1... | collective-permute-start | bytes 786440 | tf_op jit(solution)/shard_map/ppermute | solution.py:29
  52.0 11.3 %collective-permute-start.23 = (bf16[64,2048]{1,0:T(8,128)(2,1)S(1)}, bf16[64,2048]{1,0:T(8,128)(2,1)}, u32[]{:S(2)}, u32[]{:S(2)}) collective-permute-start(bf16[64,2048]{1,0:T(8,128)(2,1)S(1)} %collective-permute-done.19.refs_18_), channel_id=1, source_target_pairs={{0,8},{1,9},{2,10},{3,11},{4,12},{5,13},{6,14},{7,15},{8,0},{9,1},... | collective-permute-start | bytes 786440 | tf_op jit(solution)/shard_map/ppermute | solution.py:29
  55.1 8.9 %collective-permute-start.28 = (bf16[64,2048]{1,0:T(8,128)(2,1)S(1)}, bf16[64,2048]{1,0:T(8,128)(2,1)}, u32[]{:S(2)}, u32[]{:S(2)}) collective-permute-start(bf16[64,2048]{1,0:T(8,128)(2,1)S(1)} %collective-permute-done.20.refs_19_), channel_id=1, source_target_pairs={{0,16},{1,113},{2,18},{3,115},{4,20},{5,117},{6,22},{7,119},{8,120... | collective-permute-start | bytes 786440 | tf_op jit(solution)/shard_map/ppermute | solution.py:29
  55.3 9.1 %collective-permute-start.30 = (bf16[64,2048]{1,0:T(8,128)(2,1)S(1)}, bf16[64,2048]{1,0:T(8,128)(2,1)}, u32[]{:S(2)}, u32[]{:S(2)}) collective-permute-start(bf16[64,2048]{1,0:T(8,128)(2,1)S(1)} %collective-permute-done.20.refs_19_), channel_id=1, source_target_pairs={{0,3},{1,0},{2,1},{3,2},{4,7},{5,4},{6,5},{7,6},{8,9},{9,10},{10,1... | collective-permute-start | bytes 786440 | tf_op jit(solution)/shard_map/ppermute | solution.py:29
  57.4 7.1 %collective-permute-start.24 = (bf16[64,2048]{1,0:T(8,128)(2,1)S(1)}, bf16[64,2048]{1,0:T(8,128)(2,1)}, u32[]{:S(2)}, u32[]{:S(2)}) collective-permute-start(bf16[64,2048]{1,0:T(8,128)(2,1)S(1)} %collective-permute-done.20.refs_19_), channel_id=1, source_target_pairs={{0,8},{1,9},{2,10},{3,11},{4,12},{5,13},{6,14},{7,15},{8,0},{9,1},... | collective-permute-start | bytes 786440 | tf_op jit(solution)/shard_map/ppermute | solution.py:29
  59.6 4.3 %collective-permute-start.25 = (bf16[64,2048]{1,0:T(8,128)(2,1)S(1)}, bf16[64,2048]{1,0:T(8,128)(2,1)}, u32[]{:S(2)}, u32[]{:S(2)}) collective-permute-start(bf16[64,2048]{1,0:T(8,128)(2,1)S(1)} %collective-permute-done.21.refs_20_), channel_id=1, source_target_pairs={{0,8},{1,9},{2,10},{3,11},{4,12},{5,13},{6,14},{7,15},{8,0},{9,1},... | collective-permute-start | bytes 786440 | tf_op jit(solution)/shard_map/ppermute | solution.py:29
  59.9 15.5 %all-to-all-start = ((bf16[8,8,2048]{2,1,0:T(8,128)(2,1)}), bf16[8,8,2048]{2,1,0:T(8,128)(2,1)S(1)}, u32[]{:S(2)}, u32[]{:S(2)}) async-start(bf16[8,8,2048]{2,1,0:T(8,128)(2,1)} %bitcast.233), calls=%async_computation | async-start | bytes 524288 | tf_op jit(solution)/shard_map/all_to_all | solution.py:314
  64.0 1.9 %collective-permute-start.33 = (bf16[64,2048]{1,0:T(8,128)(2,1)S(1)}, bf16[64,2048]{1,0:T(8,128)(2,1)}, u32[]{:S(2)}, u32[]{:S(2)}) collective-permute-start(bf16[64,2048]{1,0:T(8,128)(2,1)S(1)} %collective-permute-done.29.refs_28_), channel_id=1, source_target_pairs={{0,8},{1,9},{2,10},{3,11},{4,12},{5,13},{6,14},{7,15},{8,0},{9,1},... | collective-permute-start | bytes 786440 | tf_op jit(solution)/shard_map/ppermute | solution.py:29
  64.4 1.9 %collective-permute-start.32 = (bf16[64,2048]{1,0:T(8,128)(2,1)}, bf16[64,2048]{1,0:T(8,128)(2,1)}, u32[]{:S(2)}, u32[]{:S(2)}) collective-permute-start(bf16[64,2048]{1,0:T(8,128)(2,1)} %collective-permute-done.28.refs_27_), channel_id=1, source_target_pairs={{0,8},{1,9},{2,10},{3,11},{4,12},{5,13},{6,14},{7,15},{8,0},{9,1},... | collective-permute-start | bytes 786440 | tf_op jit(solution)/shard_map/ppermute | solution.py:29
  64.5 2.2 %collective-permute-start.34 = (bf16[64,2048]{1,0:T(8,128)(2,1)}, bf16[64,2048]{1,0:T(8,128)(2,1)}, u32[]{:S(2)}, u32[]{:S(2)}) collective-permute-start(bf16[64,2048]{1,0:T(8,128)(2,1)} %collective-permute-done.30.refs_29_), channel_id=1, source_target_pairs={{0,8},{1,9},{2,10},{3,11},{4,12},{5,13},{6,14},{7,15},{8,0},{9,1},... | collective-permute-start | bytes 786440 | tf_op jit(solution)/shard_map/ppermute | solution.py:29
  102.5 4.3 %collective-permute-start.36 = (f32[2,8,128]{2,1,0:T(8,128)S(1)}, f32[2,8,128]{2,1,0:T(8,128)S(1)}, u32[]{:S(2)}, u32[]{:S(2)}) collective-permute-start(f32[2,8,128]{2,1,0:T(8,128)S(1)} %pad_maximum_fusion.6), channel_id=1, source_target_pairs={{0,8},{1,9},{2,10},{3,11},{4,12},{5,13},{6,14},{7,15},{8,0},{9,1},... | collective-permute-start | bytes 24584 | tf_op jit(solution)/shard_map/ppermute | solution.py:29
  (26 other events, 365.2 us)

commit v2 on v1

--- a/solution.py
+++ b/solution.py
@@ -38,7 +38,7 @@
 
 
 def along_x(d):
-    return {**d, "x": d["x"] + (-1 if d["c"] == 0 else 1)}
+    return {**d, "x": d["x"] + (1 if (d["x"] + d["c"]) % 2 == 0 else -1)}
 
 
 def other_core(d):
@@ -305,12 +305,18 @@
             there[k].append(moved(block, along_z))
             if step > 1:
                 back[k].append(moved(block, along_x))
+    early = []
+    for k in range(SUBS):
+        early.append(moved(blocks[k], other_core))
     parts = []
     for pair in range(0, len(hops), 2):
         group = []
         for hop in hops[pair : pair + 2]:
             group += [there[k][hop] if hop >= 0 else back[k][-hop - 1] for k in range(SUBS)]
-        parts += group + [moved(p, other_core) for p in group]
+        if pair == 0:
+            parts += group + early + [moved(p, other_core) for p in group[SUBS:]]
+        else:
+            parts += group + [moved(p, other_core) for p in group]
     got = lax.all_to_all(sent, "z", 0, 0, tiled=True)
     table_scores, stats = scored(s * half, half, embed_table, parts)
     stats, got = lax.optimization_barrier((stats, got))

time: 114 us -> 113 us (level)
  waiting for transfers between devices: 16.9 us -> 13 us
  starting transfers between devices: 48.7 us -> 52.2 us
    ppermute x35, starting transfers between devices: 45.3 us -> 48.6 us  [moved(): return lax.ppermute(block, AXES, pairs)]
    ppermute x35, waiting for transfers between devices: 14.3 us -> 12 us  [moved(): return lax.ppermute(block, AXES, pairs)]
    all_to_all x1, waiting for transfers between devices: 2.59 us -> 0.96 us  [whole(): got = lax.all_to_all(sent, 'z', 0, 0, tiled=True)]
  transfers between devices with their start and end apart: 36 -> 36, of which waited for: 14 -> 13; matrix products, arithmetic and copies ran while one was open for 7% -> 7% of each run, Pallas kernels for 5% -> 5%
where the time goes in v2:
time: 113 us
  starting transfers between devices  52.2 us (46%)
  blocking collectives  24.4 us (22%)
  waiting for transfers between devices  13 us (12%)
  Pallas kernels  11.9 us (11%)
  other arithmetic  5.66 us (5%)
  local copies, waits for them, and re-layouts  3.17 us (3%)
  matrix products  1.25 us (1%)
  between operations  1.25 us (1%)
    ppermute x35, starting transfers between devices, moved(): return lax.ppermute(block, AXES, pairs)  48.6 us
    all_to_all x2, blocking collectives, shared(): lax.all_to_all(jnp.broadcast_to(value, (count, *value.shape)), axes, 0, 0...  24.4 us
    ppermute x35, waiting for transfers between devices, moved(): return lax.ppermute(block, AXES, pairs)  12 us
    pallas_call x1, Pallas kernels, scored(): pl.pallas_call(lambda *refs: score_kernel(len(parts), refs), out_shape=[j...  6.07 us
    pallas_call x1, Pallas kernels, gradient(): pl.pallas_call(lambda *refs: gradient_kernel(len(parts), refs), out_shape...  5.78 us
    all_to_all x1, starting transfers between devices, whole(): got = lax.all_to_all(sent, 'z', 0, 0, tiled=True)  3.64 us
  transfers between devices with their start and end apart: 36, of which 13 were waited for; matrix products, arithmetic and copies ran while one was open for 7% of the time, Pallas kernels for 5%

profile of v2, /device:TPU:1, one launch (start us, length us, event | category | flops | bytes accessed | tf_op | source)
XLA Modules:
  0.0 112.8 jit_solution(4782438148015475674)
XLA Ops:
  0.0 1.1 slice_bitcast_fusion.1
  1.1 3.6 %collective-permute-start.3 = (bf16[64,2048]{1,0:T(8,128)(2,1)S(1)}, bf16[64,2048]{1,0:T(8,128)(2,1)S(1)}, u32[]{:S(2)}, u32[]{:S(2)}) collective-permute-start(bf16[64,2048]{1,0:T(8,128)(2,1)S(1)} %get-tuple-element.683), channel_id=1, source_target_pairs={{0,132},{1,133},{2,134},{3,135},{4,128},{5,129},{6,130},{7,131},{8... | collective-permute-start | bytes 786440 | tf_op jit(solution)/shard_map/ppermute | solution.py:29
  8.5 1.3 %collective-permute-done.3 = bf16[64,2048]{1,0:T(8,128)(2,1)S(1)} collective-permute-done((bf16[64,2048]{1,0:T(8,128)(2,1)S(1)}, bf16[64,2048]{1,0:T(8,128)(2,1)S(1)}, u32[]{:S(2)}, u32[]{:S(2)}) %collective-permute-start.3) | collective-permute-done | bytes 262176 | tf_op jit(solution)/shard_map/ppermute | solution.py:29
  9.8 1.0 broadcast_select_fusion.3
  10.7 4.6 %collective-permute-done.4 = bf16[64,2048]{1,0:T(8,128)(2,1)S(1)} collective-permute-done((bf16[64,2048]{1,0:T(8,128)(2,1)S(1)}, bf16[64,2048]{1,0:T(8,128)(2,1)S(1)}, u32[]{:S(2)}, u32[]{:S(2)}) %collective-permute-start.4) | collective-permute-done | bytes 262176 | tf_op jit(solution)/shard_map/ppermute | solution.py:29
  15.4 6.4 %collective-permute-start.5 = (bf16[64,2048]{1,0:T(8,128)(2,1)S(1)}, bf16[64,2048]{1,0:T(8,128)(2,1)S(1)}, u32[]{:S(2)}, u32[]{:S(2)}) collective-permute-start(bf16[64,2048]{1,0:T(8,128)(2,1)S(1)} %get-tuple-element.603.refs_2_), channel_id=1, source_target_pairs={{0,16},{1,113},{2,18},{3,115},{4,20},{5,117},{6,22},{7,119},{8,120... | collective-permute-start | bytes 786440 | tf_op jit(solution)/shard_map/ppermute | solution.py:29
  23.1 2.0 %collective-permute-done.5.refs_4_ = bf16[64,2048]{1,0:T(8,128)(2,1)S(1)} collective-permute-done((bf16[64,2048]{1,0:T(8,128)(2,1)S(1)}, bf16[64,2048]{1,0:T(8,128)(2,1)S(1)}, u32[]{:S(2)}, u32[]{:S(2)}) %collective-permute-start.5) | collective-permute-done | bytes 262176 | tf_op jit(solution)/shard_map/ppermute | solution.py:29
  25.1 3.1 %collective-permute-start.11 = (bf16[64,2048]{1,0:T(8,128)(2,1)S(1)}, bf16[64,2048]{1,0:T(8,128)(2,1)S(1)}, u32[]{:S(2)}, u32[]{:S(2)}) collective-permute-start(bf16[64,2048]{1,0:T(8,128)(2,1)S(1)} %collective-permute-done.5.refs_4_), channel_id=1, source_target_pairs={{0,16},{1,113},{2,18},{3,115},{4,20},{5,117},{6,22},{7,119},{8,120... | collective-permute-start | bytes 786440 | tf_op jit(solution)/shard_map/ppermute | solution.py:29
  29.9 1.1 collective-permute-start.12
  31.0 4.4 %collective-permute-start.10 = (bf16[64,2048]{1,0:T(8,128)(2,1)S(1)}, bf16[64,2048]{1,0:T(8,128)(2,1)S(1)}, u32[]{:S(2)}, u32[]{:S(2)}) collective-permute-start(bf16[64,2048]{1,0:T(8,128)(2,1)S(1)} %collective-permute-done.6.refs_5_), channel_id=1, source_target_pairs={{0,8},{1,9},{2,10},{3,11},{4,12},{5,13},{6,14},{7,15},{8,0},{9,1},... | collective-permute-start | bytes 786440 | tf_op jit(solution)/shard_map/ppermute | solution.py:29
  35.4 1.1 collective-permute-start.13
  36.6 1.0 convolution_convert_fusion
  38.0 2.2 %collective-permute-start.21 = (bf16[64,2048]{1,0:T(8,128)(2,1)S(1)}, bf16[64,2048]{1,0:T(8,128)(2,1)S(1)}, u32[]{:S(2)}, u32[]{:S(2)}) collective-permute-start(bf16[64,2048]{1,0:T(8,128)(2,1)S(1)} %collective-permute-done.11.refs_10_), channel_id=1, source_target_pairs={{0,1},{1,0},{2,3},{3,2},{4,5},{5,4},{6,7},{7,6},{8,11},{9,10},{10,... | collective-permute-start | bytes 786440 | tf_op jit(solution)/shard_map/ppermute | solution.py:29
  40.3 2.0 %collective-permute-start.20 = (bf16[64,2048]{1,0:T(8,128)(2,1)S(1)}, bf16[64,2048]{1,0:T(8,128)(2,1)S(1)}, u32[]{:S(2)}, u32[]{:S(2)}) collective-permute-start(bf16[64,2048]{1,0:T(8,128)(2,1)S(1)} %collective-permute-done.12.refs_11_), channel_id=1, source_target_pairs={{0,16},{1,113},{2,18},{3,115},{4,20},{5,117},{6,22},{7,119},{8,120... | collective-permute-start | bytes 786440 | tf_op jit(solution)/shard_map/ppermute | solution.py:29
  42.9 1.7 %collective-permute-start.16 = (bf16[64,2048]{1,0:T(8,128)(2,1)S(1)}, bf16[64,2048]{1,0:T(8,128)(2,1)S(1)}, u32[]{:S(2)}, u32[]{:S(2)}) collective-permute-start(bf16[64,2048]{1,0:T(8,128)(2,1)S(1)} %collective-permute-done.12.refs_11_), channel_id=1, source_target_pairs={{0,8},{1,9},{2,10},{3,11},{4,12},{5,13},{6,14},{7,15},{8,0},{9,1},... | collective-permute-start | bytes 786440 | tf_op jit(solution)/shard_map/ppermute | solution.py:29
  44.6 1.3 %collective-permute-start.18 = (bf16[64,2048]{1,0:T(8,128)(2,1)S(1)}, bf16[64,2048]{1,0:T(8,128)(2,1)S(1)}, u32[]{:S(2)}, u32[]{:S(2)}) collective-permute-start(bf16[64,2048]{1,0:T(8,128)(2,1)S(1)} %collective-permute-done.14.refs_13_), channel_id=1, source_target_pairs={{0,8},{1,9},{2,10},{3,11},{4,12},{5,13},{6,14},{7,15},{8,0},{9,1},... | collective-permute-start | bytes 786440 | tf_op jit(solution)/shard_map/ppermute | solution.py:29
  45.8 1.5 %collective-permute-start.15 = (bf16[64,2048]{1,0:T(8,128)(2,1)S(1)}, bf16[64,2048]{1,0:T(8,128)(2,1)S(1)}, u32[]{:S(2)}, u32[]{:S(2)}) collective-permute-start(bf16[64,2048]{1,0:T(8,128)(2,1)S(1)} %collective-permute-done.11.refs_10_), channel_id=1, source_target_pairs={{0,8},{1,9},{2,10},{3,11},{4,12},{5,13},{6,14},{7,15},{8,0},{9,1},... | collective-permute-start | bytes 786440 | tf_op jit(solution)/shard_map/ppermute | solution.py:29
  47.3 3.2 %collective-permute-start.17 = (bf16[64,2048]{1,0:T(8,128)(2,1)S(1)}, bf16[64,2048]{1,0:T(8,128)(2,1)S(1)}, u32[]{:S(2)}, u32[]{:S(2)}) collective-permute-start(bf16[64,2048]{1,0:T(8,128)(2,1)S(1)} %collective-permute-done.13.refs_12_), channel_id=1, source_target_pairs={{0,8},{1,9},{2,10},{3,11},{4,12},{5,13},{6,14},{7,15},{8,0},{9,1},... | collective-permute-start | bytes 786440 | tf_op jit(solution)/shard_map/ppermute | solution.py:29
  51.0 2.5 %collective-permute-start.23 = (bf16[64,2048]{1,0:T(8,128)(2,1)S(1)}, bf16[64,2048]{1,0:T(8,128)(2,1)}, u32[]{:S(2)}, u32[]{:S(2)}) collective-permute-start(bf16[64,2048]{1,0:T(8,128)(2,1)S(1)} %collective-permute-done.19.refs_18_), channel_id=1, source_target_pairs={{0,8},{1,9},{2,10},{3,11},{4,12},{5,13},{6,14},{7,15},{8,0},{9,1},... | collective-permute-start | bytes 786440 | tf_op jit(solution)/shard_map/ppermute | solution.py:29
  54.3 0.9 collective-permute-start.30
  55.2 0.9 collective-permute-done.27.refs_26_
  56.1 2.2 %collective-permute-start.24 = (bf16[64,2048]{1,0:T(8,128)(2,1)S(1)}, bf16[64,2048]{1,0:T(8,128)(2,1)}, u32[]{:S(2)}, u32[]{:S(2)}) collective-permute-start(bf16[64,2048]{1,0:T(8,128)(2,1)S(1)} %collective-permute-done.20.refs_19_), channel_id=1, source_target_pairs={{0,8},{1,9},{2,10},{3,11},{4,12},{5,13},{6,14},{7,15},{8,0},{9,1},... | collective-permute-start | bytes 786440 | tf_op jit(solution)/shard_map/ppermute | solution.py:29
  58.6 3.6 %all-to-all-start = ((bf16[8,8,2048]{2,1,0:T(8,128)(2,1)}), bf16[8,8,2048]{2,1,0:T(8,128)(2,1)S(1)}, u32[]{:S(2)}, u32[]{:S(2)}) async-start(bf16[8,8,2048]{2,1,0:T(8,128)(2,1)} %bitcast.233), calls=%async_computation | async-start | bytes 524288 | tf_op jit(solution)/shard_map/all_to_all | solution.py:320
  62.2 0.9 collective-permute-start.26
  66.0 6.1 %score.1 = (f32[256,2048]{1,0:T(8,128)S(1)}, f32[2,2048]{1,0:T(2,128)}) custom-call(s32[1]{0:T(128)} %bitcast.7.refs_0_, bf16[512,2048]{1,0:T(8,128)(2,1)} %refs_1_.1, bf16[64,2048]{1,0:T(8,128)(2,1)S(1)} %get-tuple-element.603.refs_2_, bf16[64,2048]{1,0:T(8,128)(2,1)S(1)} %get-tuple-element.679.refs_3_, bf16[64,2048]{1,0:T(8,128)(2,1)} %copy-done.1, ...), custom_call_target="tpu_custom_call" | custom-call | flops 2147483648 | bytes 9437184 | tf_op jit(solution)/shard_map/score/pallas_call | solution.py:131
  72.0 1.0 all-to-all-done
  74.0 2.2 %collective-permute-start.35 = (f32[2,8,128]{2,1,0:T(8,128)S(1)}, f32[2,8,128]{2,1,0:T(8,128)S(1)}, u32[]{:S(2)}, u32[]{:S(2)}) collective-permute-start(f32[2,8,128]{2,1,0:T(8,128)S(1)} %pad_maximum_fusion.3), channel_id=1, source_target_pairs={{0,8},{1,9},{2,10},{3,11},{4,12},{5,13},{6,14},{7,15},{8,0},{9,1},... | collective-permute-start | bytes 24584 | tf_op jit(solution)/shard_map/ppermute | solution.py:29
  77.0 13.2 %all_to_all.22 = f32[16,2,8,128]{3,2,1,0:T(8,128)S(1)} all-to-all(f32[16,2,8,128]{3,2,1,0:T(8,128)S(1)} %broadcast_in_dim.244), channel_id=1, replica_groups=mesh['s'=2,'z'=8,'c'=2,'u'=2,'x'=4] {'s','u','x'}, dimensions={0} | all-to-all | bytes 262144 | tf_op jit(solution)/shard_map/all_to_all | solution.py:60
  90.2 11.2 %all_to_all.23 = f32[8,2,8,128]{3,2,1,0:T(8,128)S(1)} all-to-all(f32[8,2,8,128]{3,2,1,0:T(8,128)S(1)} %broadcast_in_dim.245), channel_id=1, replica_groups=mesh['s'=2,'z'=8,'c'=2,'u'=2,'x'=4] {'z'}, dimensions={0} | all-to-all | bytes 131072 | tf_op jit(solution)/shard_map/all_to_all | solution.py:60
  101.5 3.3 %collective-permute-start.36 = (f32[2,8,128]{2,1,0:T(8,128)S(1)}, f32[2,8,128]{2,1,0:T(8,128)S(1)}, u32[]{:S(2)}, u32[]{:S(2)}) collective-permute-start(f32[2,8,128]{2,1,0:T(8,128)S(1)} %pad_maximum_fusion.6), channel_id=1, source_target_pairs={{0,8},{1,9},{2,10},{3,11},{4,12},{5,13},{6,14},{7,15},{8,0},{9,1},... | collective-permute-start | bytes 24584 | tf_op jit(solution)/shard_map/ppermute | solution.py:29
  106.8 5.8 %conditional.1 = (bf16[1,1,256,2048]{3,2,1,0:T(8,128)(2,1)}) conditional(s32[]{:T(128)} %convert_element_type.63, (s32[]{:T(128)}, f32[1,2048]{1,0:T(1,128)S(1)}, s32[1,2048]{1,0:T(1,128)S(1)}, s32[1,128]{1,0:T(1,128)S(1)}, bf16[64,2048]{1,0:T(8,128)(2,1)S(1)}, /*index=5*/bf16[64,2048]{1,0:T(8,128)(2,1)}, f32[256,2048]{1,0:T(8,128)S(1)}, ...), branch_computations={%region_22.23_spmd, %region_23.26_spmd} | conditional | flops 2417656064 | bytes 35751588 | solution.py:366
  106.8 5.8 %gradient.2 = bf16[256,2048]{1,0:T(8,128)(2,1)} custom-call(s32[1]{0:T(128)} %bitcast.refs_0_, f32[1,2048]{1,0:T(1,128)S(1)} %get-tuple-element.490.refs_1_, s32[1,2048]{1,0:T(1,128)S(1)} %get-tuple-element.491.refs_2_, s32[1,128]{1,0:T(1,128)S(1)} %get-tuple-element.492.refs_3_, bf16[64,2048]{1,0:T(8,128)(2,1)S(1)} %get-tuple-element.493.refs_4_, ...), custom_call_target="tpu_custom_call" | custom-call | flops 2147483648 | bytes 8388608 | tf_op jit(solution)/shard_map/cond/branch_0_fun/gradient/pallas_call | solution.py:201
  (145 shorter events, 15.4 us)
Async XLA Ops:
  1.1 8.6 %collective-permute-start.3 = (bf16[64,2048]{1,0:T(8,128)(2,1)S(1)}, bf16[64,2048]{1,0:T(8,128)(2,1)S(1)}, u32[]{:S(2)}, u32[]{:S(2)}) collective-permute-start(bf16[64,2048]{1,0:T(8,128)(2,1)S(1)} %get-tuple-element.683), channel_id=1, source_target_pairs={{0,132},{1,133},{2,134},{3,135},{4,128},{5,129},{6,130},{7,131},{8... | collective-permute-start | bytes 786440 | tf_op jit(solution)/shard_map/ppermute | solution.py:29
  4.8 10.6 %collective-permute-start.4 = (bf16[64,2048]{1,0:T(8,128)(2,1)S(1)}, bf16[64,2048]{1,0:T(8,128)(2,1)S(1)}, u32[]{:S(2)}, u32[]{:S(2)}) collective-permute-start(bf16[64,2048]{1,0:T(8,128)(2,1)S(1)} %get-tuple-element.684), channel_id=1, source_target_pairs={{0,132},{1,133},{2,134},{3,135},{4,128},{5,129},{6,130},{7,131},{8... | collective-permute-start | bytes 786440 | tf_op jit(solution)/shard_map/ppermute | solution.py:29
  15.4 9.7 %collective-permute-start.5 = (bf16[64,2048]{1,0:T(8,128)(2,1)S(1)}, bf16[64,2048]{1,0:T(8,128)(2,1)S(1)}, u32[]{:S(2)}, u32[]{:S(2)}) collective-permute-start(bf16[64,2048]{1,0:T(8,128)(2,1)S(1)} %get-tuple-element.603.refs_2_), channel_id=1, source_target_pairs={{0,16},{1,113},{2,18},{3,115},{4,20},{5,117},{6,22},{7,119},{8,120... | collective-permute-start | bytes 786440 | tf_op jit(solution)/shard_map/ppermute | solution.py:29
  21.8 8.1 %collective-permute-start.6 = (bf16[64,2048]{1,0:T(8,128)(2,1)S(1)}, bf16[64,2048]{1,0:T(8,128)(2,1)S(1)}, u32[]{:S(2)}, u32[]{:S(2)}) collective-permute-start(bf16[64,2048]{1,0:T(8,128)(2,1)S(1)} %get-tuple-element.679.refs_3_), channel_id=1, source_target_pairs={{0,16},{1,113},{2,18},{3,115},{4,20},{5,117},{6,22},{7,119},{8,120... | collective-permute-start | bytes 786440 | tf_op jit(solution)/shard_map/ppermute | solution.py:29
  22.6 8.4 %collective-permute-start.8 = (bf16[64,2048]{1,0:T(8,128)(2,1)S(1)}, bf16[64,2048]{1,0:T(8,128)(2,1)S(1)}, u32[]{:S(2)}, u32[]{:S(2)}) collective-permute-start(bf16[64,2048]{1,0:T(8,128)(2,1)S(1)} %get-tuple-element.679.refs_3_), channel_id=1, source_target_pairs={{0,8},{1,9},{2,10},{3,11},{4,12},{5,13},{6,14},{7,15},{8,0},{9,1},... | collective-permute-start | bytes 786440 | tf_op jit(solution)/shard_map/ppermute | solution.py:29
  22.6 12.8 %collective-permute-start.7 = (bf16[64,2048]{1,0:T(8,128)(2,1)S(1)}, bf16[64,2048]{1,0:T(8,128)(2,1)S(1)}, u32[]{:S(2)}, u32[]{:S(2)}) collective-permute-start(bf16[64,2048]{1,0:T(8,128)(2,1)S(1)} %get-tuple-element.603.refs_2_), channel_id=1, source_target_pairs={{0,8},{1,9},{2,10},{3,11},{4,12},{5,13},{6,14},{7,15},{8,0},{9,1},... | collective-permute-start | bytes 786440 | tf_op jit(solution)/shard_map/ppermute | solution.py:29
  25.1 11.4 %collective-permute-start.11 = (bf16[64,2048]{1,0:T(8,128)(2,1)S(1)}, bf16[64,2048]{1,0:T(8,128)(2,1)S(1)}, u32[]{:S(2)}, u32[]{:S(2)}) collective-permute-start(bf16[64,2048]{1,0:T(8,128)(2,1)S(1)} %collective-permute-done.5.refs_4_), channel_id=1, source_target_pairs={{0,16},{1,113},{2,18},{3,115},{4,20},{5,117},{6,22},{7,119},{8,120... | collective-permute-start | bytes 786440 | tf_op jit(solution)/shard_map/ppermute | solution.py:29
  29.9 7.6 %collective-permute-start.12 = (bf16[64,2048]{1,0:T(8,128)(2,1)S(1)}, bf16[64,2048]{1,0:T(8,128)(2,1)S(1)}, u32[]{:S(2)}, u32[]{:S(2)}) collective-permute-start(bf16[64,2048]{1,0:T(8,128)(2,1)S(1)} %collective-permute-done.6.refs_5_), channel_id=1, source_target_pairs={{0,16},{1,113},{2,18},{3,115},{4,20},{5,117},{6,22},{7,119},{8,120... | collective-permute-start | bytes 786440 | tf_op jit(solution)/shard_map/ppermute | solution.py:29
  31.0 7.0 %collective-permute-start.14 = (bf16[64,2048]{1,0:T(8,128)(2,1)S(1)}, bf16[64,2048]{1,0:T(8,128)(2,1)S(1)}, u32[]{:S(2)}, u32[]{:S(2)}) collective-permute-start(bf16[64,2048]{1,0:T(8,128)(2,1)S(1)} %collective-permute-done.6.refs_5_), channel_id=1, source_target_pairs={{0,1},{1,0},{2,3},{3,2},{4,5},{5,4},{6,7},{7,6},{8,11},{9,10},{10,... | collective-permute-start | bytes 786440 | tf_op jit(solution)/shard_map/ppermute | solution.py:29
  31.0 9.2 %collective-permute-start.10 = (bf16[64,2048]{1,0:T(8,128)(2,1)S(1)}, bf16[64,2048]{1,0:T(8,128)(2,1)S(1)}, u32[]{:S(2)}, u32[]{:S(2)}) collective-permute-start(bf16[64,2048]{1,0:T(8,128)(2,1)S(1)} %collective-permute-done.6.refs_5_), channel_id=1, source_target_pairs={{0,8},{1,9},{2,10},{3,11},{4,12},{5,13},{6,14},{7,15},{8,0},{9,1},... | collective-permute-start | bytes 786440 | tf_op jit(solution)/shard_map/ppermute | solution.py:29
  35.4 6.9 %collective-permute-start.13 = (bf16[64,2048]{1,0:T(8,128)(2,1)S(1)}, bf16[64,2048]{1,0:T(8,128)(2,1)S(1)}, u32[]{:S(2)}, u32[]{:S(2)}) collective-permute-start(bf16[64,2048]{1,0:T(8,128)(2,1)S(1)} %collective-permute-done.5.refs_4_), channel_id=1, source_target_pairs={{0,1},{1,0},{2,3},{3,2},{4,5},{5,4},{6,7},{7,6},{8,11},{9,10},{10,... | collective-permute-start | bytes 786440 | tf_op jit(solution)/shard_map/ppermute | solution.py:29
  36.5 6.4 %collective-permute-start.9 = (bf16[64,2048]{1,0:T(8,128)(2,1)S(1)}, bf16[64,2048]{1,0:T(8,128)(2,1)S(1)}, u32[]{:S(2)}, u32[]{:S(2)}) collective-permute-start(bf16[64,2048]{1,0:T(8,128)(2,1)S(1)} %collective-permute-done.5.refs_4_), channel_id=1, source_target_pairs={{0,8},{1,9},{2,10},{3,11},{4,12},{5,13},{6,14},{7,15},{8,0},{9,1},... | collective-permute-start | bytes 786440 | tf_op jit(solution)/shard_map/ppermute | solution.py:29
  37.5 7.0 %collective-permute-start.19 = (bf16[64,2048]{1,0:T(8,128)(2,1)S(1)}, bf16[64,2048]{1,0:T(8,128)(2,1)S(1)}, u32[]{:S(2)}, u32[]{:S(2)}) collective-permute-start(bf16[64,2048]{1,0:T(8,128)(2,1)S(1)} %collective-permute-done.11.refs_10_), channel_id=1, source_target_pairs={{0,16},{1,113},{2,18},{3,115},{4,20},{5,117},{6,22},{7,119},{8,120... | collective-permute-start | bytes 786440 | tf_op jit(solution)/shard_map/ppermute | solution.py:29
  38.0 7.8 %collective-permute-start.21 = (bf16[64,2048]{1,0:T(8,128)(2,1)S(1)}, bf16[64,2048]{1,0:T(8,128)(2,1)S(1)}, u32[]{:S(2)}, u32[]{:S(2)}) collective-permute-start(bf16[64,2048]{1,0:T(8,128)(2,1)S(1)} %collective-permute-done.11.refs_10_), channel_id=1, source_target_pairs={{0,1},{1,0},{2,3},{3,2},{4,5},{5,4},{6,7},{7,6},{8,11},{9,10},{10,... | collective-permute-start | bytes 786440 | tf_op jit(solution)/shard_map/ppermute | solution.py:29
  40.3 7.1 %collective-permute-start.20 = (bf16[64,2048]{1,0:T(8,128)(2,1)S(1)}, bf16[64,2048]{1,0:T(8,128)(2,1)S(1)}, u32[]{:S(2)}, u32[]{:S(2)}) collective-permute-start(bf16[64,2048]{1,0:T(8,128)(2,1)S(1)} %collective-permute-done.12.refs_11_), channel_id=1, source_target_pairs={{0,16},{1,113},{2,18},{3,115},{4,20},{5,117},{6,22},{7,119},{8,120... | collective-permute-start | bytes 786440 | tf_op jit(solution)/shard_map/ppermute | solution.py:29
  42.3 8.3 %collective-permute-start.22 = (bf16[64,2048]{1,0:T(8,128)(2,1)S(1)}, bf16[64,2048]{1,0:T(8,128)(2,1)S(1)}, u32[]{:S(2)}, u32[]{:S(2)}) collective-permute-start(bf16[64,2048]{1,0:T(8,128)(2,1)S(1)} %collective-permute-done.12.refs_11_), channel_id=1, source_target_pairs={{0,1},{1,0},{2,3},{3,2},{4,5},{5,4},{6,7},{7,6},{8,11},{9,10},{10,... | collective-permute-start | bytes 786440 | tf_op jit(solution)/shard_map/ppermute | solution.py:29
  42.9 7.7 %collective-permute-start.16 = (bf16[64,2048]{1,0:T(8,128)(2,1)S(1)}, bf16[64,2048]{1,0:T(8,128)(2,1)S(1)}, u32[]{:S(2)}, u32[]{:S(2)}) collective-permute-start(bf16[64,2048]{1,0:T(8,128)(2,1)S(1)} %collective-permute-done.12.refs_11_), channel_id=1, source_target_pairs={{0,8},{1,9},{2,10},{3,11},{4,12},{5,13},{6,14},{7,15},{8,0},{9,1},... | collective-permute-start | bytes 786440 | tf_op jit(solution)/shard_map/ppermute | solution.py:29
  44.6 6.4 %collective-permute-start.18 = (bf16[64,2048]{1,0:T(8,128)(2,1)S(1)}, bf16[64,2048]{1,0:T(8,128)(2,1)S(1)}, u32[]{:S(2)}, u32[]{:S(2)}) collective-permute-start(bf16[64,2048]{1,0:T(8,128)(2,1)S(1)} %collective-permute-done.14.refs_13_), channel_id=1, source_target_pairs={{0,8},{1,9},{2,10},{3,11},{4,12},{5,13},{6,14},{7,15},{8,0},{9,1},... | collective-permute-start | bytes 786440 | tf_op jit(solution)/shard_map/ppermute | solution.py:29
  45.8 7.6 %collective-permute-start.15 = (bf16[64,2048]{1,0:T(8,128)(2,1)S(1)}, bf16[64,2048]{1,0:T(8,128)(2,1)S(1)}, u32[]{:S(2)}, u32[]{:S(2)}) collective-permute-start(bf16[64,2048]{1,0:T(8,128)(2,1)S(1)} %collective-permute-done.11.refs_10_), channel_id=1, source_target_pairs={{0,8},{1,9},{2,10},{3,11},{4,12},{5,13},{6,14},{7,15},{8,0},{9,1},... | collective-permute-start | bytes 786440 | tf_op jit(solution)/shard_map/ppermute | solution.py:29
  47.3 7.0 %collective-permute-start.17 = (bf16[64,2048]{1,0:T(8,128)(2,1)S(1)}, bf16[64,2048]{1,0:T(8,128)(2,1)S(1)}, u32[]{:S(2)}, u32[]{:S(2)}) collective-permute-start(bf16[64,2048]{1,0:T(8,128)(2,1)S(1)} %collective-permute-done.13.refs_12_), channel_id=1, source_target_pairs={{0,8},{1,9},{2,10},{3,11},{4,12},{5,13},{6,14},{7,15},{8,0},{9,1},... | collective-permute-start | bytes 786440 | tf_op jit(solution)/shard_map/ppermute | solution.py:29
  50.6 5.5 %collective-permute-start.27 = (bf16[64,2048]{1,0:T(8,128)(2,1)S(1)}, bf16[64,2048]{1,0:T(8,128)(2,1)S(1)}, u32[]{:S(2)}, u32[]{:S(2)}) collective-permute-start(bf16[64,2048]{1,0:T(8,128)(2,1)S(1)} %collective-permute-done.19.refs_18_), channel_id=1, source_target_pairs={{0,16},{1,113},{2,18},{3,115},{4,20},{5,117},{6,22},{7,119},{8,120... | collective-permute-start | bytes 786440 | tf_op jit(solution)/shard_map/ppermute | solution.py:29
  50.6 7.7 %collective-permute-start.29 = (bf16[64,2048]{1,0:T(8,128)(2,1)S(1)}, bf16[64,2048]{1,0:T(8,128)(2,1)S(1)}, u32[]{:S(2)}, u32[]{:S(2)}) collective-permute-start(bf16[64,2048]{1,0:T(8,128)(2,1)S(1)} %collective-permute-done.19.refs_18_), channel_id=1, source_target_pairs={{0,1},{1,0},{2,3},{3,2},{4,5},{5,4},{6,7},{7,6},{8,11},{9,10},{10,... | collective-permute-start | bytes 786440 | tf_op jit(solution)/shard_map/ppermute | solution.py:29
  51.0 11.3 %collective-permute-start.23 = (bf16[64,2048]{1,0:T(8,128)(2,1)S(1)}, bf16[64,2048]{1,0:T(8,128)(2,1)}, u32[]{:S(2)}, u32[]{:S(2)}) collective-permute-start(bf16[64,2048]{1,0:T(8,128)(2,1)S(1)} %collective-permute-done.19.refs_18_), channel_id=1, source_target_pairs={{0,8},{1,9},{2,10},{3,11},{4,12},{5,13},{6,14},{7,15},{8,0},{9,1},... | collective-permute-start | bytes 786440 | tf_op jit(solution)/shard_map/ppermute | solution.py:29
  53.5 9.7 %collective-permute-start.28 = (bf16[64,2048]{1,0:T(8,128)(2,1)S(1)}, bf16[64,2048]{1,0:T(8,128)(2,1)}, u32[]{:S(2)}, u32[]{:S(2)}) collective-permute-start(bf16[64,2048]{1,0:T(8,128)(2,1)S(1)} %collective-permute-done.20.refs_19_), channel_id=1, source_target_pairs={{0,16},{1,113},{2,18},{3,115},{4,20},{5,117},{6,22},{7,119},{8,120... | collective-permute-start | bytes 786440 | tf_op jit(solution)/shard_map/ppermute | solution.py:29
  54.3 9.3 %collective-permute-start.30 = (bf16[64,2048]{1,0:T(8,128)(2,1)S(1)}, bf16[64,2048]{1,0:T(8,128)(2,1)}, u32[]{:S(2)}, u32[]{:S(2)}) collective-permute-start(bf16[64,2048]{1,0:T(8,128)(2,1)S(1)} %collective-permute-done.20.refs_19_), channel_id=1, source_target_pairs={{0,1},{1,0},{2,3},{3,2},{4,5},{5,4},{6,7},{7,6},{8,11},{9,10},{10,... | collective-permute-start | bytes 786440 | tf_op jit(solution)/shard_map/ppermute | solution.py:29
  56.1 7.6 %collective-permute-start.24 = (bf16[64,2048]{1,0:T(8,128)(2,1)S(1)}, bf16[64,2048]{1,0:T(8,128)(2,1)}, u32[]{:S(2)}, u32[]{:S(2)}) collective-permute-start(bf16[64,2048]{1,0:T(8,128)(2,1)S(1)} %collective-permute-done.20.refs_19_), channel_id=1, source_target_pairs={{0,8},{1,9},{2,10},{3,11},{4,12},{5,13},{6,14},{7,15},{8,0},{9,1},... | collective-permute-start | bytes 786440 | tf_op jit(solution)/shard_map/ppermute | solution.py:29
  58.3 4.8 %collective-permute-start.25 = (bf16[64,2048]{1,0:T(8,128)(2,1)S(1)}, bf16[64,2048]{1,0:T(8,128)(2,1)}, u32[]{:S(2)}, u32[]{:S(2)}) collective-permute-start(bf16[64,2048]{1,0:T(8,128)(2,1)S(1)} %collective-permute-done.21.refs_20_), channel_id=1, source_target_pairs={{0,8},{1,9},{2,10},{3,11},{4,12},{5,13},{6,14},{7,15},{8,0},{9,1},... | collective-permute-start | bytes 786440 | tf_op jit(solution)/shard_map/ppermute | solution.py:29
  58.6 14.4 %all-to-all-start = ((bf16[8,8,2048]{2,1,0:T(8,128)(2,1)}), bf16[8,8,2048]{2,1,0:T(8,128)(2,1)S(1)}, u32[]{:S(2)}, u32[]{:S(2)}) async-start(bf16[8,8,2048]{2,1,0:T(8,128)(2,1)} %bitcast.233), calls=%async_computation | async-start | bytes 524288 | tf_op jit(solution)/shard_map/all_to_all | solution.py:320
  62.2 2.1 %collective-permute-start.26 = (bf16[64,2048]{1,0:T(8,128)(2,1)S(1)}, bf16[64,2048]{1,0:T(8,128)(2,1)}, u32[]{:S(2)}, u32[]{:S(2)}) collective-permute-start(bf16[64,2048]{1,0:T(8,128)(2,1)S(1)} %collective-permute-done.22.refs_21_), channel_id=1, source_target_pairs={{0,8},{1,9},{2,10},{3,11},{4,12},{5,13},{6,14},{7,15},{8,0},{9,1},... | collective-permute-start | bytes 786440 | tf_op jit(solution)/shard_map/ppermute | solution.py:29
  63.7 2.2 %collective-permute-start.34 = (bf16[64,2048]{1,0:T(8,128)(2,1)}, bf16[64,2048]{1,0:T(8,128)(2,1)}, u32[]{:S(2)}, u32[]{:S(2)}) collective-permute-start(bf16[64,2048]{1,0:T(8,128)(2,1)} %collective-permute-done.30.refs_29_), channel_id=1, source_target_pairs={{0,8},{1,9},{2,10},{3,11},{4,12},{5,13},{6,14},{7,15},{8,0},{9,1},... | collective-permute-start | bytes 786440 | tf_op jit(solution)/shard_map/ppermute | solution.py:29
  74.0 3.0 %collective-permute-start.35 = (f32[2,8,128]{2,1,0:T(8,128)S(1)}, f32[2,8,128]{2,1,0:T(8,128)S(1)}, u32[]{:S(2)}, u32[]{:S(2)}) collective-permute-start(f32[2,8,128]{2,1,0:T(8,128)S(1)} %pad_maximum_fusion.3), channel_id=1, source_target_pairs={{0,8},{1,9},{2,10},{3,11},{4,12},{5,13},{6,14},{7,15},{8,0},{9,1},... | collective-permute-start | bytes 24584 | tf_op jit(solution)/shard_map/ppermute | solution.py:29
  101.5 4.1 %collective-permute-start.36 = (f32[2,8,128]{2,1,0:T(8,128)S(1)}, f32[2,8,128]{2,1,0:T(8,128)S(1)}, u32[]{:S(2)}, u32[]{:S(2)}) collective-permute-start(f32[2,8,128]{2,1,0:T(8,128)S(1)} %pad_maximum_fusion.6), channel_id=1, source_target_pairs={{0,8},{1,9},{2,10},{3,11},{4,12},{5,13},{6,14},{7,15},{8,0},{9,1},... | collective-permute-start | bytes 24584 | tf_op jit(solution)/shard_map/ppermute | solution.py:29
  (26 other events, 364.5 us)

commit v3 on v2

--- a/solution.py
+++ b/solution.py
@@ -328,10 +328,13 @@
     inverse = jnp.sum(jnp.where(order[None, :] == place[:, None], place[None, :], 0), axis=1)
     near = jnp.stack([picked(local[0], inverse[:nz]), picked(local[1], inverse[:nz])])
     far = jnp.stack([picked(local[0], inverse[nz:]), picked(local[1], inverse[nz:])])
-    pair = joined(jnp.stack([near, moved(far, other_core)]))
-    pair = joined(shared(pair, ("s", "u", "x")))
-    pair = joined(shared(pair, "z"))
-    pair = jnp.concatenate([pair, moved(pair, other_core)], axis=1)
+    each = jnp.stack([jnp.where(c == core, near, far) for core in range(2)])
+    fan = (n["s"], nc, n["u"] * n["x"], *near.shape)
+    each = jnp.broadcast_to(each[None, :, None], fan).reshape(-1, *near.shape)
+    pair = joined(lax.all_to_all(each, ("s", "c", "u", "x"), 0, 0, tiled=True))
+    both = shared(pair, ("z", "c")).reshape(nz, nc, *pair.shape)
+    both = jnp.where(c == 0, both, both[:, ::-1])
+    pair = jnp.concatenate([joined(both[:, core]) for core in range(2)], axis=1)
     factor = jnp.exp(local[0] - picked(pair[0], order)) / picked(pair[1], order)
     factor = factor.reshape(1, shards * rows)
 

time: 113 us -> 115 us (1.018)
  blocking collectives: 24.4 us -> 17.5 us
  waiting for transfers between devices: 13 us -> 19.1 us
  other arithmetic: 5.66 us -> 7.57 us
  starting transfers between devices: 52.2 us -> 50.8 us
  local copies, waits for them, and re-layouts: 3.17 us -> 4.34 us
    all_to_all x0 -> x1, waiting for transfers between devices: none -> 8.15 us  [shared(): lax.all_to_all(jnp.broadcast_to(value, (count, *value.shape)), axes, 0, 0...]
    all_to_all x2 -> x1, blocking collectives: 24.4 us -> 17.5 us  [whole(): pair = joined(lax.all_to_all(each, ('s', 'c', 'u', 'x'), 0, 0, tiled=True))]
    ppermute x35 -> x33, starting transfers between devices: 48.6 us -> 42.3 us  [moved(): return lax.ppermute(block, AXES, pairs)]
    all_to_all x0 -> x1, starting transfers between devices: none -> 4.92 us  [shared(): lax.all_to_all(jnp.broadcast_to(value, (count, *value.shape)), axes, 0, 0...]
    ppermute x35 -> x33, waiting for transfers between devices: 12 us -> 10 us  [moved(): return lax.ppermute(block, AXES, pairs)]
    reduce_sum x4, other arithmetic: 0.45 us -> 1.71 us  [picked(): jnp.sum(jnp.where(hit, table[None], jnp.zeros((), table.dtype)), axis=1)]
  transfers between devices with their start and end apart: 36 -> 35, of which waited for: 13 -> 11; matrix products, arithmetic and copies ran while one was open for 7% -> 9% of each run, Pallas kernels for 5% -> 5%
where the time goes in v3:
time: 115 us
  starting transfers between devices  50.8 us (44%)
  waiting for transfers between devices  19.1 us (17%)
  blocking collectives  17.5 us (15%)
  Pallas kernels  12.6 us (11%)
  other arithmetic  7.57 us (7%)
  local copies, waits for them, and re-layouts  4.34 us (4%)
  between operations  1.28 us (1%)
  matrix products  1.26 us (1%)
    ppermute x33, starting transfers between devices, moved(): return lax.ppermute(block, AXES, pairs)  42.3 us
    all_to_all x1, blocking collectives, whole(): pair = joined(lax.all_to_all(each, ('s', 'c', 'u', 'x'), 0, 0, tiled=True))  17.5 us
    ppermute x33, waiting for transfers between devices, moved(): return lax.ppermute(block, AXES, pairs)  10 us
    all_to_all x1, waiting for transfers between devices, shared(): lax.all_to_all(jnp.broadcast_to(value, (count, *value.shape)), axes, 0, 0...  8.15 us
    pallas_call x1, Pallas kernels, gradient(): pl.pallas_call(lambda *refs: gradient_kernel(len(parts), refs), out_shape...  6.54 us
    pallas_call x1, Pallas kernels, scored(): pl.pallas_call(lambda *refs: score_kernel(len(parts), refs), out_shape=[j...  6.07 us
    all_to_all x1, starting transfers between devices, shared(): lax.all_to_all(jnp.broadcast_to(value, (count, *value.shape)), axes, 0, 0...  4.92 us
    all_to_all x1, starting transfers between devices, whole(): got = lax.all_to_all(sent, 'z', 0, 0, tiled=True)  3.56 us
  transfers between devices with their start and end apart: 35, of which 11 were waited for; matrix products, arithmetic and copies ran while one was open for 9% of the time, Pallas kernels for 5%

profile of v3, /device:TPU:1, one launch (start us, length us, event | category | flops | bytes accessed | tf_op | source)
XLA Modules:
  0.0 114.7 jit_solution(1759526618976195190)
XLA Ops:
  0.0 1.1 slice_bitcast_fusion.1
  1.1 3.6 %collective-permute-start.3 = (bf16[64,2048]{1,0:T(8,128)(2,1)S(1)}, bf16[64,2048]{1,0:T(8,128)(2,1)S(1)}, u32[]{:S(2)}, u32[]{:S(2)}) collective-permute-start(bf16[64,2048]{1,0:T(8,128)(2,1)S(1)} %get-tuple-element.683), channel_id=1, source_target_pairs={{0,132},{1,133},{2,134},{3,135},{4,128},{5,129},{6,130},{7,131},{8... | collective-permute-start | bytes 786440 | tf_op jit(solution)/shard_map/ppermute | solution.py:29
  8.5 1.3 %collective-permute-done.3 = bf16[64,2048]{1,0:T(8,128)(2,1)S(1)} collective-permute-done((bf16[64,2048]{1,0:T(8,128)(2,1)S(1)}, bf16[64,2048]{1,0:T(8,128)(2,1)S(1)}, u32[]{:S(2)}, u32[]{:S(2)}) %collective-permute-start.3) | collective-permute-done | bytes 262176 | tf_op jit(solution)/shard_map/ppermute | solution.py:29
  9.8 1.0 broadcast_select_fusion.3
  10.8 4.6 %collective-permute-done.4 = bf16[64,2048]{1,0:T(8,128)(2,1)S(1)} collective-permute-done((bf16[64,2048]{1,0:T(8,128)(2,1)S(1)}, bf16[64,2048]{1,0:T(8,128)(2,1)S(1)}, u32[]{:S(2)}, u32[]{:S(2)}) %collective-permute-start.4) | collective-permute-done | bytes 262176 | tf_op jit(solution)/shard_map/ppermute | solution.py:29
  15.4 6.4 %collective-permute-start.5 = (bf16[64,2048]{1,0:T(8,128)(2,1)S(1)}, bf16[64,2048]{1,0:T(8,128)(2,1)S(1)}, u32[]{:S(2)}, u32[]{:S(2)}) collective-permute-start(bf16[64,2048]{1,0:T(8,128)(2,1)S(1)} %get-tuple-element.603.refs_2_), channel_id=1, source_target_pairs={{0,16},{1,113},{2,18},{3,115},{4,20},{5,117},{6,22},{7,119},{8,120... | collective-permute-start | bytes 786440 | tf_op jit(solution)/shard_map/ppermute | solution.py:29
  23.1 2.0 %collective-permute-done.5.refs_4_ = bf16[64,2048]{1,0:T(8,128)(2,1)S(1)} collective-permute-done((bf16[64,2048]{1,0:T(8,128)(2,1)S(1)}, bf16[64,2048]{1,0:T(8,128)(2,1)S(1)}, u32[]{:S(2)}, u32[]{:S(2)}) %collective-permute-start.5) | collective-permute-done | bytes 262176 | tf_op jit(solution)/shard_map/ppermute | solution.py:29
  25.1 3.1 %collective-permute-start.11 = (bf16[64,2048]{1,0:T(8,128)(2,1)S(1)}, bf16[64,2048]{1,0:T(8,128)(2,1)S(1)}, u32[]{:S(2)}, u32[]{:S(2)}) collective-permute-start(bf16[64,2048]{1,0:T(8,128)(2,1)S(1)} %collective-permute-done.5.refs_4_), channel_id=1, source_target_pairs={{0,16},{1,113},{2,18},{3,115},{4,20},{5,117},{6,22},{7,119},{8,120... | collective-permute-start | bytes 786440 | tf_op jit(solution)/shard_map/ppermute | solution.py:29
  31.1 4.4 %collective-permute-start.10 = (bf16[64,2048]{1,0:T(8,128)(2,1)S(1)}, bf16[64,2048]{1,0:T(8,128)(2,1)S(1)}, u32[]{:S(2)}, u32[]{:S(2)}) collective-permute-start(bf16[64,2048]{1,0:T(8,128)(2,1)S(1)} %collective-permute-done.6.refs_5_), channel_id=1, source_target_pairs={{0,8},{1,9},{2,10},{3,11},{4,12},{5,13},{6,14},{7,15},{8,0},{9,1},... | collective-permute-start | bytes 786440 | tf_op jit(solution)/shard_map/ppermute | solution.py:29
  35.5 1.1 collective-permute-start.13
  36.7 1.0 convolution_convert_fusion
  38.1 3.2 %collective-permute-start.21 = (bf16[64,2048]{1,0:T(8,128)(2,1)S(1)}, bf16[64,2048]{1,0:T(8,128)(2,1)S(1)}, u32[]{:S(2)}, u32[]{:S(2)}) collective-permute-start(bf16[64,2048]{1,0:T(8,128)(2,1)S(1)} %collective-permute-done.11.refs_10_), channel_id=1, source_target_pairs={{0,1},{1,0},{2,3},{3,2},{4,5},{5,4},{6,7},{7,6},{8,11},{9,10},{10,... | collective-permute-start | bytes 786440 | tf_op jit(solution)/shard_map/ppermute | solution.py:29
  41.3 1.1 collective-permute-start.20
  43.0 1.6 %collective-permute-start.16 = (bf16[64,2048]{1,0:T(8,128)(2,1)S(1)}, bf16[64,2048]{1,0:T(8,128)(2,1)S(1)}, u32[]{:S(2)}, u32[]{:S(2)}) collective-permute-start(bf16[64,2048]{1,0:T(8,128)(2,1)S(1)} %collective-permute-done.12.refs_11_), channel_id=1, source_target_pairs={{0,8},{1,9},{2,10},{3,11},{4,12},{5,13},{6,14},{7,15},{8,0},{9,1},... | collective-permute-start | bytes 786440 | tf_op jit(solution)/shard_map/ppermute | solution.py:29
  44.7 1.2 %collective-permute-start.18 = (bf16[64,2048]{1,0:T(8,128)(2,1)S(1)}, bf16[64,2048]{1,0:T(8,128)(2,1)S(1)}, u32[]{:S(2)}, u32[]{:S(2)}) collective-permute-start(bf16[64,2048]{1,0:T(8,128)(2,1)S(1)} %collective-permute-done.14.refs_13_), channel_id=1, source_target_pairs={{0,8},{1,9},{2,10},{3,11},{4,12},{5,13},{6,14},{7,15},{8,0},{9,1},... | collective-permute-start | bytes 786440 | tf_op jit(solution)/shard_map/ppermute | solution.py:29
  45.8 1.5 %collective-permute-start.15 = (bf16[64,2048]{1,0:T(8,128)(2,1)S(1)}, bf16[64,2048]{1,0:T(8,128)(2,1)S(1)}, u32[]{:S(2)}, u32[]{:S(2)}) collective-permute-start(bf16[64,2048]{1,0:T(8,128)(2,1)S(1)} %collective-permute-done.11.refs_10_), channel_id=1, source_target_pairs={{0,8},{1,9},{2,10},{3,11},{4,12},{5,13},{6,14},{7,15},{8,0},{9,1},... | collective-permute-start | bytes 786440 | tf_op jit(solution)/shard_map/ppermute | solution.py:29
  47.3 3.3 %collective-permute-start.17 = (bf16[64,2048]{1,0:T(8,128)(2,1)S(1)}, bf16[64,2048]{1,0:T(8,128)(2,1)S(1)}, u32[]{:S(2)}, u32[]{:S(2)}) collective-permute-start(bf16[64,2048]{1,0:T(8,128)(2,1)S(1)} %collective-permute-done.13.refs_12_), channel_id=1, source_target_pairs={{0,8},{1,9},{2,10},{3,11},{4,12},{5,13},{6,14},{7,15},{8,0},{9,1},... | collective-permute-start | bytes 786440 | tf_op jit(solution)/shard_map/ppermute | solution.py:29
  50.7 1.4 %collective-permute-start.29 = (bf16[64,2048]{1,0:T(8,128)(2,1)S(1)}, bf16[64,2048]{1,0:T(8,128)(2,1)S(1)}, u32[]{:S(2)}, u32[]{:S(2)}) collective-permute-start(bf16[64,2048]{1,0:T(8,128)(2,1)S(1)} %collective-permute-done.19.refs_18_), channel_id=1, source_target_pairs={{0,1},{1,0},{2,3},{3,2},{4,5},{5,4},{6,7},{7,6},{8,11},{9,10},{10,... | collective-permute-start | bytes 786440 | tf_op jit(solution)/shard_map/ppermute | solution.py:29
  52.1 1.4 %collective-permute-start.23 = (bf16[64,2048]{1,0:T(8,128)(2,1)S(1)}, bf16[64,2048]{1,0:T(8,128)(2,1)}, u32[]{:S(2)}, u32[]{:S(2)}) collective-permute-start(bf16[64,2048]{1,0:T(8,128)(2,1)S(1)} %collective-permute-done.19.refs_18_), channel_id=1, source_target_pairs={{0,8},{1,9},{2,10},{3,11},{4,12},{5,13},{6,14},{7,15},{8,0},{9,1},... | collective-permute-start | bytes 786440 | tf_op jit(solution)/shard_map/ppermute | solution.py:29
  53.5 1.2 %collective-permute-start.28 = (bf16[64,2048]{1,0:T(8,128)(2,1)S(1)}, bf16[64,2048]{1,0:T(8,128)(2,1)}, u32[]{:S(2)}, u32[]{:S(2)}) collective-permute-start(bf16[64,2048]{1,0:T(8,128)(2,1)S(1)} %collective-permute-done.20.refs_19_), channel_id=1, source_target_pairs={{0,16},{1,113},{2,18},{3,115},{4,20},{5,117},{6,22},{7,119},{8,120... | collective-permute-start | bytes 786440 | tf_op jit(solution)/shard_map/ppermute | solution.py:29
  54.8 1.0 collective-permute-start.30
  56.2 2.2 %collective-permute-start.24 = (bf16[64,2048]{1,0:T(8,128)(2,1)S(1)}, bf16[64,2048]{1,0:T(8,128)(2,1)}, u32[]{:S(2)}, u32[]{:S(2)}) collective-permute-start(bf16[64,2048]{1,0:T(8,128)(2,1)S(1)} %collective-permute-done.20.refs_19_), channel_id=1, source_target_pairs={{0,8},{1,9},{2,10},{3,11},{4,12},{5,13},{6,14},{7,15},{8,0},{9,1},... | collective-permute-start | bytes 786440 | tf_op jit(solution)/shard_map/ppermute | solution.py:29
  58.7 3.6 %all-to-all-start = ((bf16[8,8,2048]{2,1,0:T(8,128)(2,1)}), bf16[8,8,2048]{2,1,0:T(8,128)(2,1)S(1)}, u32[]{:S(2)}, u32[]{:S(2)}) async-start(bf16[8,8,2048]{2,1,0:T(8,128)(2,1)} %bitcast.236), calls=%async_computation | async-start | bytes 524288 | tf_op jit(solution)/shard_map/all_to_all | solution.py:320
  62.3 0.9 collective-permute-start.26
  66.0 6.1 %score.1 = (f32[256,2048]{1,0:T(8,128)S(1)}, f32[2,2048]{1,0:T(2,128)}) custom-call(s32[1]{0:T(128)} %bitcast.7.refs_0_, bf16[512,2048]{1,0:T(8,128)(2,1)} %refs_1_.1, bf16[64,2048]{1,0:T(8,128)(2,1)S(1)} %get-tuple-element.603.refs_2_, bf16[64,2048]{1,0:T(8,128)(2,1)S(1)} %get-tuple-element.679.refs_3_, bf16[64,2048]{1,0:T(8,128)(2,1)} %copy-done.1, ...), custom_call_target="tpu_custom_call" | custom-call | flops 2147483648 | bytes 9437184 | tf_op jit(solution)/shard_map/score/pallas_call | solution.py:131
  72.1 1.0 all-to-all-done
  73.0 0.8 fusion.165
  74.0 17.5 %all_to_all.22 = f32[32,2,8,128]{3,2,1,0:T(8,128)S(1)} all-to-all(f32[32,2,8,128]{3,2,1,0:T(8,128)S(1)} %bitcast.237), channel_id=1, replica_groups=mesh['s'=2,'z'=8,'c'=2,'u'=2,'x'=4] {'s','c','u','x'}, dimensions={0} | all-to-all | bytes 524288 | tf_op jit(solution)/shard_map/all_to_all | solution.py:334
  92.2 4.9 %all-to-all-start.2 = ((f32[16,2,8,128]{3,2,1,0:T(8,128)}), f32[16,2,8,128]{3,2,1,0:T(8,128)S(1)}, u32[]{:S(2)}, u32[]{:S(2)}) async-start(f32[16,2,8,128]{3,2,1,0:T(8,128)} %broadcast_in_dim.248), calls=%async_computation.2 | async-start | bytes 262144 | tf_op jit(solution)/shard_map/all_to_all | solution.py:60
  97.9 8.1 %all-to-all-done.2 = f32[16,2,8,128]{3,2,1,0:T(8,128)S(1)} async-done(((f32[16,2,8,128]{3,2,1,0:T(8,128)}), f32[16,2,8,128]{3,2,1,0:T(8,128)S(1)}, u32[]{:S(2)}, u32[]{:S(2)}) %all-to-all-start.2) | async-done | bytes 131104 | tf_op jit(solution)/shard_map/all_to_all | solution.py:60
  107.7 6.8 %conditional.1 = (bf16[1,1,256,2048]{3,2,1,0:T(8,128)(2,1)}) conditional(s32[]{:T(128)} %convert_element_type.63, (s32[]{:T(128)}, f32[1,2048]{1,0:T(1,128)S(1)}, s32[1,2048]{1,0:T(1,128)}, s32[1,128]{1,0:T(1,128)}, bf16[64,2048]{1,0:T(8,128)(2,1)S(1)}, /*index=5*/bf16[64,2048]{1,0:T(8,128)(2,1)}, f32[256,2048]{1,0:T(8,128)S(1)}, ...), branch_computations={%region_22.23_spmd, %region_23.26_spmd} | conditional | flops 2417656064 | bytes 35882688 | solution.py:369
  108.0 6.5 %gradient.2 = bf16[256,2048]{1,0:T(8,128)(2,1)} custom-call(s32[1]{0:T(128)} %bitcast.refs_0_, f32[1,2048]{1,0:T(1,128)S(1)} %get-tuple-element.490.refs_1_, s32[1,2048]{1,0:T(1,128)} %get-tuple-element.491.refs_2_, s32[1,128]{1,0:T(1,128)} %get-tuple-element.492.refs_3_, bf16[64,2048]{1,0:T(8,128)(2,1)S(1)} %get-tuple-element.493.refs_4_, ...), custom_call_target="tpu_custom_call" | custom-call | flops 2147483648 | bytes 8388608 | tf_op jit(solution)/shard_map/cond/branch_0_fun/gradient/pallas_call | solution.py:201
  (144 shorter events, 15.2 us)
Async XLA Ops:
  1.1 8.6 %collective-permute-start.3 = (bf16[64,2048]{1,0:T(8,128)(2,1)S(1)}, bf16[64,2048]{1,0:T(8,128)(2,1)S(1)}, u32[]{:S(2)}, u32[]{:S(2)}) collective-permute-start(bf16[64,2048]{1,0:T(8,128)(2,1)S(1)} %get-tuple-element.683), channel_id=1, source_target_pairs={{0,132},{1,133},{2,134},{3,135},{4,128},{5,129},{6,130},{7,131},{8... | collective-permute-start | bytes 786440 | tf_op jit(solution)/shard_map/ppermute | solution.py:29
  4.8 10.6 %collective-permute-start.4 = (bf16[64,2048]{1,0:T(8,128)(2,1)S(1)}, bf16[64,2048]{1,0:T(8,128)(2,1)S(1)}, u32[]{:S(2)}, u32[]{:S(2)}) collective-permute-start(bf16[64,2048]{1,0:T(8,128)(2,1)S(1)} %get-tuple-element.684), channel_id=1, source_target_pairs={{0,132},{1,133},{2,134},{3,135},{4,128},{5,129},{6,130},{7,131},{8... | collective-permute-start | bytes 786440 | tf_op jit(solution)/shard_map/ppermute | solution.py:29
  15.4 9.7 %collective-permute-start.5 = (bf16[64,2048]{1,0:T(8,128)(2,1)S(1)}, bf16[64,2048]{1,0:T(8,128)(2,1)S(1)}, u32[]{:S(2)}, u32[]{:S(2)}) collective-permute-start(bf16[64,2048]{1,0:T(8,128)(2,1)S(1)} %get-tuple-element.603.refs_2_), channel_id=1, source_target_pairs={{0,16},{1,113},{2,18},{3,115},{4,20},{5,117},{6,22},{7,119},{8,120... | collective-permute-start | bytes 786440 | tf_op jit(solution)/shard_map/ppermute | solution.py:29
  21.8 9.2 %collective-permute-start.6 = (bf16[64,2048]{1,0:T(8,128)(2,1)S(1)}, bf16[64,2048]{1,0:T(8,128)(2,1)S(1)}, u32[]{:S(2)}, u32[]{:S(2)}) collective-permute-start(bf16[64,2048]{1,0:T(8,128)(2,1)S(1)} %get-tuple-element.679.refs_3_), channel_id=1, source_target_pairs={{0,16},{1,113},{2,18},{3,115},{4,20},{5,117},{6,22},{7,119},{8,120... | collective-permute-start | bytes 786440 | tf_op jit(solution)/shard_map/ppermute | solution.py:29
  22.6 8.5 %collective-permute-start.8 = (bf16[64,2048]{1,0:T(8,128)(2,1)S(1)}, bf16[64,2048]{1,0:T(8,128)(2,1)S(1)}, u32[]{:S(2)}, u32[]{:S(2)}) collective-permute-start(bf16[64,2048]{1,0:T(8,128)(2,1)S(1)} %get-tuple-element.679.refs_3_), channel_id=1, source_target_pairs={{0,8},{1,9},{2,10},{3,11},{4,12},{5,13},{6,14},{7,15},{8,0},{9,1},... | collective-permute-start | bytes 786440 | tf_op jit(solution)/shard_map/ppermute | solution.py:29
  22.6 12.9 %collective-permute-start.7 = (bf16[64,2048]{1,0:T(8,128)(2,1)S(1)}, bf16[64,2048]{1,0:T(8,128)(2,1)S(1)}, u32[]{:S(2)}, u32[]{:S(2)}) collective-permute-start(bf16[64,2048]{1,0:T(8,128)(2,1)S(1)} %get-tuple-element.603.refs_2_), channel_id=1, source_target_pairs={{0,8},{1,9},{2,10},{3,11},{4,12},{5,13},{6,14},{7,15},{8,0},{9,1},... | collective-permute-start | bytes 786440 | tf_op jit(solution)/shard_map/ppermute | solution.py:29
  25.1 11.5 %collective-permute-start.11 = (bf16[64,2048]{1,0:T(8,128)(2,1)S(1)}, bf16[64,2048]{1,0:T(8,128)(2,1)S(1)}, u32[]{:S(2)}, u32[]{:S(2)}) collective-permute-start(bf16[64,2048]{1,0:T(8,128)(2,1)S(1)} %collective-permute-done.5.refs_4_), channel_id=1, source_target_pairs={{0,16},{1,113},{2,18},{3,115},{4,20},{5,117},{6,22},{7,119},{8,120... | collective-permute-start | bytes 786440 | tf_op jit(solution)/shard_map/ppermute | solution.py:29
  31.0 6.7 %collective-permute-start.12 = (bf16[64,2048]{1,0:T(8,128)(2,1)S(1)}, bf16[64,2048]{1,0:T(8,128)(2,1)S(1)}, u32[]{:S(2)}, u32[]{:S(2)}) collective-permute-start(bf16[64,2048]{1,0:T(8,128)(2,1)S(1)} %collective-permute-done.6.refs_5_), channel_id=1, source_target_pairs={{0,16},{1,113},{2,18},{3,115},{4,20},{5,117},{6,22},{7,119},{8,120... | collective-permute-start | bytes 786440 | tf_op jit(solution)/shard_map/ppermute | solution.py:29
  31.0 7.1 %collective-permute-start.14 = (bf16[64,2048]{1,0:T(8,128)(2,1)S(1)}, bf16[64,2048]{1,0:T(8,128)(2,1)S(1)}, u32[]{:S(2)}, u32[]{:S(2)}) collective-permute-start(bf16[64,2048]{1,0:T(8,128)(2,1)S(1)} %collective-permute-done.6.refs_5_), channel_id=1, source_target_pairs={{0,1},{1,0},{2,3},{3,2},{4,5},{5,4},{6,7},{7,6},{8,11},{9,10},{10,... | collective-permute-start | bytes 786440 | tf_op jit(solution)/shard_map/ppermute | solution.py:29
  31.1 10.2 %collective-permute-start.10 = (bf16[64,2048]{1,0:T(8,128)(2,1)S(1)}, bf16[64,2048]{1,0:T(8,128)(2,1)S(1)}, u32[]{:S(2)}, u32[]{:S(2)}) collective-permute-start(bf16[64,2048]{1,0:T(8,128)(2,1)S(1)} %collective-permute-done.6.refs_5_), channel_id=1, source_target_pairs={{0,8},{1,9},{2,10},{3,11},{4,12},{5,13},{6,14},{7,15},{8,0},{9,1},... | collective-permute-start | bytes 786440 | tf_op jit(solution)/shard_map/ppermute | solution.py:29
  35.5 6.9 %collective-permute-start.13 = (bf16[64,2048]{1,0:T(8,128)(2,1)S(1)}, bf16[64,2048]{1,0:T(8,128)(2,1)S(1)}, u32[]{:S(2)}, u32[]{:S(2)}) collective-permute-start(bf16[64,2048]{1,0:T(8,128)(2,1)S(1)} %collective-permute-done.5.refs_4_), channel_id=1, source_target_pairs={{0,1},{1,0},{2,3},{3,2},{4,5},{5,4},{6,7},{7,6},{8,11},{9,10},{10,... | collective-permute-start | bytes 786440 | tf_op jit(solution)/shard_map/ppermute | solution.py:29
  36.6 6.4 %collective-permute-start.9 = (bf16[64,2048]{1,0:T(8,128)(2,1)S(1)}, bf16[64,2048]{1,0:T(8,128)(2,1)S(1)}, u32[]{:S(2)}, u32[]{:S(2)}) collective-permute-start(bf16[64,2048]{1,0:T(8,128)(2,1)S(1)} %collective-permute-done.5.refs_4_), channel_id=1, source_target_pairs={{0,8},{1,9},{2,10},{3,11},{4,12},{5,13},{6,14},{7,15},{8,0},{9,1},... | collective-permute-start | bytes 786440 | tf_op jit(solution)/shard_map/ppermute | solution.py:29
  37.7 7.0 %collective-permute-start.19 = (bf16[64,2048]{1,0:T(8,128)(2,1)S(1)}, bf16[64,2048]{1,0:T(8,128)(2,1)S(1)}, u32[]{:S(2)}, u32[]{:S(2)}) collective-permute-start(bf16[64,2048]{1,0:T(8,128)(2,1)S(1)} %collective-permute-done.11.refs_10_), channel_id=1, source_target_pairs={{0,16},{1,113},{2,18},{3,115},{4,20},{5,117},{6,22},{7,119},{8,120... | collective-permute-start | bytes 786440 | tf_op jit(solution)/shard_map/ppermute | solution.py:29
  38.1 7.7 %collective-permute-start.21 = (bf16[64,2048]{1,0:T(8,128)(2,1)S(1)}, bf16[64,2048]{1,0:T(8,128)(2,1)S(1)}, u32[]{:S(2)}, u32[]{:S(2)}) collective-permute-start(bf16[64,2048]{1,0:T(8,128)(2,1)S(1)} %collective-permute-done.11.refs_10_), channel_id=1, source_target_pairs={{0,1},{1,0},{2,3},{3,2},{4,5},{5,4},{6,7},{7,6},{8,11},{9,10},{10,... | collective-permute-start | bytes 786440 | tf_op jit(solution)/shard_map/ppermute | solution.py:29
  41.3 6.0 %collective-permute-start.20 = (bf16[64,2048]{1,0:T(8,128)(2,1)S(1)}, bf16[64,2048]{1,0:T(8,128)(2,1)S(1)}, u32[]{:S(2)}, u32[]{:S(2)}) collective-permute-start(bf16[64,2048]{1,0:T(8,128)(2,1)S(1)} %collective-permute-done.12.refs_11_), channel_id=1, source_target_pairs={{0,16},{1,113},{2,18},{3,115},{4,20},{5,117},{6,22},{7,119},{8,120... | collective-permute-start | bytes 786440 | tf_op jit(solution)/shard_map/ppermute | solution.py:29
  42.4 8.2 %collective-permute-start.22 = (bf16[64,2048]{1,0:T(8,128)(2,1)S(1)}, bf16[64,2048]{1,0:T(8,128)(2,1)S(1)}, u32[]{:S(2)}, u32[]{:S(2)}) collective-permute-start(bf16[64,2048]{1,0:T(8,128)(2,1)S(1)} %collective-permute-done.12.refs_11_), channel_id=1, source_target_pairs={{0,1},{1,0},{2,3},{3,2},{4,5},{5,4},{6,7},{7,6},{8,11},{9,10},{10,... | collective-permute-start | bytes 786440 | tf_op jit(solution)/shard_map/ppermute | solution.py:29
  43.0 7.6 %collective-permute-start.16 = (bf16[64,2048]{1,0:T(8,128)(2,1)S(1)}, bf16[64,2048]{1,0:T(8,128)(2,1)S(1)}, u32[]{:S(2)}, u32[]{:S(2)}) collective-permute-start(bf16[64,2048]{1,0:T(8,128)(2,1)S(1)} %collective-permute-done.12.refs_11_), channel_id=1, source_target_pairs={{0,8},{1,9},{2,10},{3,11},{4,12},{5,13},{6,14},{7,15},{8,0},{9,1},... | collective-permute-start | bytes 786440 | tf_op jit(solution)/shard_map/ppermute | solution.py:29
  44.7 7.4 %collective-permute-start.18 = (bf16[64,2048]{1,0:T(8,128)(2,1)S(1)}, bf16[64,2048]{1,0:T(8,128)(2,1)S(1)}, u32[]{:S(2)}, u32[]{:S(2)}) collective-permute-start(bf16[64,2048]{1,0:T(8,128)(2,1)S(1)} %collective-permute-done.14.refs_13_), channel_id=1, source_target_pairs={{0,8},{1,9},{2,10},{3,11},{4,12},{5,13},{6,14},{7,15},{8,0},{9,1},... | collective-permute-start | bytes 786440 | tf_op jit(solution)/shard_map/ppermute | solution.py:29
  45.8 7.6 %collective-permute-start.15 = (bf16[64,2048]{1,0:T(8,128)(2,1)S(1)}, bf16[64,2048]{1,0:T(8,128)(2,1)S(1)}, u32[]{:S(2)}, u32[]{:S(2)}) collective-permute-start(bf16[64,2048]{1,0:T(8,128)(2,1)S(1)} %collective-permute-done.11.refs_10_), channel_id=1, source_target_pairs={{0,8},{1,9},{2,10},{3,11},{4,12},{5,13},{6,14},{7,15},{8,0},{9,1},... | collective-permute-start | bytes 786440 | tf_op jit(solution)/shard_map/ppermute | solution.py:29
  47.3 7.4 %collective-permute-start.17 = (bf16[64,2048]{1,0:T(8,128)(2,1)S(1)}, bf16[64,2048]{1,0:T(8,128)(2,1)S(1)}, u32[]{:S(2)}, u32[]{:S(2)}) collective-permute-start(bf16[64,2048]{1,0:T(8,128)(2,1)S(1)} %collective-permute-done.13.refs_12_), channel_id=1, source_target_pairs={{0,8},{1,9},{2,10},{3,11},{4,12},{5,13},{6,14},{7,15},{8,0},{9,1},... | collective-permute-start | bytes 786440 | tf_op jit(solution)/shard_map/ppermute | solution.py:29
  50.7 5.5 %collective-permute-start.27 = (bf16[64,2048]{1,0:T(8,128)(2,1)S(1)}, bf16[64,2048]{1,0:T(8,128)(2,1)S(1)}, u32[]{:S(2)}, u32[]{:S(2)}) collective-permute-start(bf16[64,2048]{1,0:T(8,128)(2,1)S(1)} %collective-permute-done.19.refs_18_), channel_id=1, source_target_pairs={{0,16},{1,113},{2,18},{3,115},{4,20},{5,117},{6,22},{7,119},{8,120... | collective-permute-start | bytes 786440 | tf_op jit(solution)/shard_map/ppermute | solution.py:29
  50.7 7.7 %collective-permute-start.29 = (bf16[64,2048]{1,0:T(8,128)(2,1)S(1)}, bf16[64,2048]{1,0:T(8,128)(2,1)S(1)}, u32[]{:S(2)}, u32[]{:S(2)}) collective-permute-start(bf16[64,2048]{1,0:T(8,128)(2,1)S(1)} %collective-permute-done.19.refs_18_), channel_id=1, source_target_pairs={{0,1},{1,0},{2,3},{3,2},{4,5},{5,4},{6,7},{7,6},{8,11},{9,10},{10,... | collective-permute-start | bytes 786440 | tf_op jit(solution)/shard_map/ppermute | solution.py:29
  52.1 10.2 %collective-permute-start.23 = (bf16[64,2048]{1,0:T(8,128)(2,1)S(1)}, bf16[64,2048]{1,0:T(8,128)(2,1)}, u32[]{:S(2)}, u32[]{:S(2)}) collective-permute-start(bf16[64,2048]{1,0:T(8,128)(2,1)S(1)} %collective-permute-done.19.refs_18_), channel_id=1, source_target_pairs={{0,8},{1,9},{2,10},{3,11},{4,12},{5,13},{6,14},{7,15},{8,0},{9,1},... | collective-permute-start | bytes 786440 | tf_op jit(solution)/shard_map/ppermute | solution.py:29
  53.5 9.7 %collective-permute-start.28 = (bf16[64,2048]{1,0:T(8,128)(2,1)S(1)}, bf16[64,2048]{1,0:T(8,128)(2,1)}, u32[]{:S(2)}, u32[]{:S(2)}) collective-permute-start(bf16[64,2048]{1,0:T(8,128)(2,1)S(1)} %collective-permute-done.20.refs_19_), channel_id=1, source_target_pairs={{0,16},{1,113},{2,18},{3,115},{4,20},{5,117},{6,22},{7,119},{8,120... | collective-permute-start | bytes 786440 | tf_op jit(solution)/shard_map/ppermute | solution.py:29
  54.8 8.9 %collective-permute-start.30 = (bf16[64,2048]{1,0:T(8,128)(2,1)S(1)}, bf16[64,2048]{1,0:T(8,128)(2,1)}, u32[]{:S(2)}, u32[]{:S(2)}) collective-permute-start(bf16[64,2048]{1,0:T(8,128)(2,1)S(1)} %collective-permute-done.20.refs_19_), channel_id=1, source_target_pairs={{0,1},{1,0},{2,3},{3,2},{4,5},{5,4},{6,7},{7,6},{8,11},{9,10},{10,... | collective-permute-start | bytes 786440 | tf_op jit(solution)/shard_map/ppermute | solution.py:29
  56.2 7.6 %collective-permute-start.24 = (bf16[64,2048]{1,0:T(8,128)(2,1)S(1)}, bf16[64,2048]{1,0:T(8,128)(2,1)}, u32[]{:S(2)}, u32[]{:S(2)}) collective-permute-start(bf16[64,2048]{1,0:T(8,128)(2,1)S(1)} %collective-permute-done.20.refs_19_), channel_id=1, source_target_pairs={{0,8},{1,9},{2,10},{3,11},{4,12},{5,13},{6,14},{7,15},{8,0},{9,1},... | collective-permute-start | bytes 786440 | tf_op jit(solution)/shard_map/ppermute | solution.py:29
  58.4 4.7 %collective-permute-start.25 = (bf16[64,2048]{1,0:T(8,128)(2,1)S(1)}, bf16[64,2048]{1,0:T(8,128)(2,1)}, u32[]{:S(2)}, u32[]{:S(2)}) collective-permute-start(bf16[64,2048]{1,0:T(8,128)(2,1)S(1)} %collective-permute-done.21.refs_20_), channel_id=1, source_target_pairs={{0,8},{1,9},{2,10},{3,11},{4,12},{5,13},{6,14},{7,15},{8,0},{9,1},... | collective-permute-start | bytes 786440 | tf_op jit(solution)/shard_map/ppermute | solution.py:29
  58.7 14.3 %all-to-all-start = ((bf16[8,8,2048]{2,1,0:T(8,128)(2,1)}), bf16[8,8,2048]{2,1,0:T(8,128)(2,1)S(1)}, u32[]{:S(2)}, u32[]{:S(2)}) async-start(bf16[8,8,2048]{2,1,0:T(8,128)(2,1)} %bitcast.236), calls=%async_computation | async-start | bytes 524288 | tf_op jit(solution)/shard_map/all_to_all | solution.py:320
  62.3 2.1 %collective-permute-start.26 = (bf16[64,2048]{1,0:T(8,128)(2,1)S(1)}, bf16[64,2048]{1,0:T(8,128)(2,1)}, u32[]{:S(2)}, u32[]{:S(2)}) collective-permute-start(bf16[64,2048]{1,0:T(8,128)(2,1)S(1)} %collective-permute-done.22.refs_21_), channel_id=1, source_target_pairs={{0,8},{1,9},{2,10},{3,11},{4,12},{5,13},{6,14},{7,15},{8,0},{9,1},... | collective-permute-start | bytes 786440 | tf_op jit(solution)/shard_map/ppermute | solution.py:29
  63.7 2.2 %collective-permute-start.34 = (bf16[64,2048]{1,0:T(8,128)(2,1)}, bf16[64,2048]{1,0:T(8,128)(2,1)}, u32[]{:S(2)}, u32[]{:S(2)}) collective-permute-start(bf16[64,2048]{1,0:T(8,128)(2,1)} %collective-permute-done.30.refs_29_), channel_id=1, source_target_pairs={{0,8},{1,9},{2,10},{3,11},{4,12},{5,13},{6,14},{7,15},{8,0},{9,1},... | collective-permute-start | bytes 786440 | tf_op jit(solution)/shard_map/ppermute | solution.py:29
  92.2 13.8 %all-to-all-start.2 = ((f32[16,2,8,128]{3,2,1,0:T(8,128)}), f32[16,2,8,128]{3,2,1,0:T(8,128)S(1)}, u32[]{:S(2)}, u32[]{:S(2)}) async-start(f32[16,2,8,128]{3,2,1,0:T(8,128)} %broadcast_in_dim.248), calls=%async_computation.2 | async-start | bytes 262144 | tf_op jit(solution)/shard_map/all_to_all | solution.py:60
  97.8 9.9 %collective-permute-start.35 = (bf16[64,2048]{1,0:T(8,128)(2,1)S(1)}, bf16[64,2048]{1,0:T(8,128)(2,1)}, u32[]{:S(2)}, u32[]{:S(2)}) collective-permute-start(bf16[64,2048]{1,0:T(8,128)(2,1)S(1)} %bitcast.232), channel_id=1, source_target_pairs={{0,8},{1,9},{2,10},{3,11},{4,12},{5,13},{6,14},{7,15},{8,0},{9,1},... | collective-permute-start | bytes 786440 | tf_op jit(solution)/shard_map/ppermute | solution.py:29
  (26 other events, 388.5 us)
